TPU v7x, 32 devices: a 4x2x2 block of a 4x4x8 slice. The times are simulated.
32 devices in a mesh: dp: 4 (over y, z), tp: 8 (over x, core).
Axes of the slice: x: 4, y: 2, z: 2, core: 2. Of those that a mesh axis runs over, the one named last changes fastest.
The devices are a block of a 4x4x8 slice.
Arguments:
- x: bfloat16 [8, 512, 4096], P('dp', 'tp'), parts along dimension 0
- start: int32 [8], P('dp'), parts along dimension 0
- k_local: bfloat16 [8, 4096, 8, 128], P('dp', None, 'tp'), parts along dimension 0
- v_local: bfloat16 [8, 4096, 8, 128], P('dp', None, 'tp'), parts along dimension 0
- k_global: bfloat16 [8, 4608, 8, 128], P('dp', None, 'tp'), parts along dimension 0
- v_global: bfloat16 [8, 4608, 8, 128], P('dp', None, 'tp'), parts along dimension 0
- norms: float32 [2, 4, 4096], replicated
- w_q: bfloat16 [2, 4096, 4096], P(None, None, 'tp')
- w_k: bfloat16 [2, 4096, 1024], P(None, None, 'tp')
- w_v: bfloat16 [2, 4096, 1024], P(None, None, 'tp')
- w_o: bfloat16 [2, 4096, 4096], P(None, 'tp')
- w_gate: bfloat16 [2, 4096, 14336], P(None, None, 'tp')
- w_up: bfloat16 [2, 4096, 14336], P(None, None, 'tp')
- w_down: bfloat16 [2, 14336, 4096], P(None, 'tp')
Outputs:
- output 1: bfloat16 [8, 512, 4096], P('dp', 'tp'), parts along dimension 0
- output 2: bfloat16 [8, 4096, 8, 128], P('dp', None, 'tp'), parts along dimension 0
- output 3: bfloat16 [8, 4096, 8, 128], P('dp', None, 'tp'), parts along dimension 0
- output 4: bfloat16 [8, 4608, 8, 128], P('dp', None, 'tp'), parts along dimension 0
- output 5: bfloat16 [8, 4608, 8, 128], P('dp', None, 'tp'), parts along dimension 0
There are 4 independent parts. A program takes and returns all parts, laid end to end along the dimension named above; an argument that names none is the same for every part.
All inputs are finite; a program needn't handle non-finite values.
Results may differ from a plain program's by a relative error of at most 0.02.
Values are sent between devices in bfloat16 or wider.
A program may use at most 768 MiB of HBM per device.

v0:
```python
import jax
import jax.numpy as jnp
from jax import lax
from jax.sharding import PartitionSpec as P

SOFT_CAP = 50.0
NORM_EPS = 1e-6
ROPE_BASE = 10000.0


def rms_norm(hidden, scale):
    hidden_f32 = hidden.astype(jnp.float32)
    inv_rms = lax.rsqrt(jnp.mean(hidden_f32 * hidden_f32, axis=-1, keepdims=True) + NORM_EPS)
    return hidden_f32 * inv_rms * (1.0 + scale)


def rope_apply(projected, positions):
    half_dim = projected.shape[-1] // 2
    inv_freq = ROPE_BASE ** (jnp.arange(half_dim, dtype=jnp.float32) * (-2.0 / projected.shape[-1]))
    angles = positions.astype(jnp.float32)[..., None] * inv_freq
    cos_tab = jnp.cos(angles)[..., None, :]
    sin_tab = jnp.sin(angles)[..., None, :]
    lead_half = projected[..., :half_dim]
    tail_half = projected[..., half_dim:]
    return jnp.concatenate([lead_half * cos_tab - tail_half * sin_tab, tail_half * cos_tab + lead_half * sin_tab], axis=-1)


def window_positions(start, window):
    slot_ids = jnp.arange(window, dtype=jnp.int32)
    last_pos = start[:, None] - 1
    return last_pos - jnp.remainder(last_pos - slot_ids[None, :], window)


def window_write(cache, fresh, start):
    window = cache.shape[1]
    chunk_len = fresh.shape[1]
    keep_len = min(chunk_len, window)
    tail_rows = jnp.pad(fresh[:, chunk_len - keep_len:], ((0, 0), (0, window - keep_len), (0, 0), (0, 0)))
    first_pos = start + (chunk_len - keep_len)
    rolled = jax.vmap(lambda rows, amount: jnp.roll(rows, amount, axis=0))(tail_rows, jnp.remainder(first_pos, window))
    slot_ids = jnp.arange(window, dtype=jnp.int32)
    written = jnp.remainder(slot_ids[None, :] - first_pos[:, None], window) < keep_len
    return jnp.where(written[:, :, None, None], rolled, cache)


def linear_write(cache, fresh, start):
    return jax.vmap(lambda rows, new_rows, offset: lax.dynamic_update_slice(rows, new_rows, (offset, 0, 0)))(cache, fresh, start)


def attend_seq(q_seq, k_seq, v_seq, q_pos, k_pos, window):
    chunk_len, heads, head_dim = q_seq.shape
    kv_heads = k_seq.shape[1]
    block_rows = min(chunk_len, 64)
    q_scale = head_dim ** -0.5
    q_blocks = q_seq.reshape(chunk_len // block_rows, block_rows, kv_heads, heads // kv_heads, head_dim)
    pos_blocks = q_pos.reshape(chunk_len // block_rows, block_rows)

    def one_block(item):
        q_blk, p_blk = item
        scores = jnp.einsum('qkgd,tkd->kgqt', q_blk, k_seq, preferred_element_type=jnp.float32) * q_scale
        capped = SOFT_CAP * jnp.tanh(scores / SOFT_CAP)
        allowed = k_pos[None, :] <= p_blk[:, None]
        if window > 0:
            allowed = allowed & (k_pos[None, :] > p_blk[:, None] - window) & (k_pos[None, :] >= 0)
        masked = jnp.where(allowed, capped, -1e30)
        weights = jnp.exp(masked - jnp.max(masked, axis=-1, keepdims=True))
        probs = (weights / jnp.sum(weights, axis=-1, keepdims=True)).astype(jnp.bfloat16)
        block_out = jnp.einsum('kgqt,tkd->qkgd', probs, v_seq, preferred_element_type=jnp.float32)
        return block_out.astype(jnp.bfloat16)

    all_blocks = lax.map(one_block, (q_blocks, pos_blocks))
    return all_blocks.reshape(chunk_len, heads * head_dim)


def attention_half(x_rows, positions, start, k_cache, v_cache, norm_pre, norm_post, w_q, w_k, w_v, w_o, is_local):
    num_seqs = x_rows.shape[0]
    head_dim = k_cache.shape[3]
    normed = rms_norm(x_rows, norm_pre).astype(jnp.bfloat16)
    gathered = lax.all_gather(normed, 'tp', axis=1, tiled=True)
    chunk_len = gathered.shape[1]
    q_proj = jnp.einsum('bcd,dn->bcn', gathered, w_q, preferred_element_type=jnp.float32)
    k_proj = jnp.einsum('bcd,dn->bcn', gathered, w_k, preferred_element_type=jnp.float32)
    v_proj = jnp.einsum('bcd,dn->bcn', gathered, w_v, preferred_element_type=jnp.float32)
    q_rot = rope_apply(q_proj.reshape(num_seqs, chunk_len, -1, head_dim), positions).astype(jnp.bfloat16)
    k_new = rope_apply(k_proj.reshape(num_seqs, chunk_len, -1, head_dim), positions).astype(jnp.bfloat16)
    v_new = v_proj.reshape(num_seqs, chunk_len, -1, head_dim).astype(jnp.bfloat16)
    if is_local:
        window = k_cache.shape[1]
        k_keys = jnp.concatenate([k_cache, k_new], axis=1)
        v_keys = jnp.concatenate([v_cache, v_new], axis=1)
        key_pos = jnp.concatenate([window_positions(start, window), positions], axis=1)
        k_next = window_write(k_cache, k_new, start)
        v_next = window_write(v_cache, v_new, start)
    else:
        window = 0
        k_next = linear_write(k_cache, k_new, start)
        v_next = linear_write(v_cache, v_new, start)
        k_keys = k_next
        v_keys = v_next
        key_pos = jnp.broadcast_to(jnp.arange(k_cache.shape[1], dtype=jnp.int32)[None, :], (num_seqs, k_cache.shape[1]))
    mixed = lax.map(lambda item: attend_seq(item[0], item[1], item[2], item[3], item[4], window), (q_rot, k_keys, v_keys, positions, key_pos))
    part_sum = jnp.einsum('bcn,nd->bcd', mixed, w_o, preferred_element_type=jnp.float32).astype(jnp.bfloat16)
    attn_rows = lax.psum_scatter(part_sum, 'tp', scatter_dimension=1, tiled=True)
    x_next = (x_rows.astype(jnp.float32) + rms_norm(attn_rows, norm_post)).astype(jnp.bfloat16)
    return x_next, k_next, v_next


def mlp_half(x_rows, norm_pre, norm_post, w_gate, w_up, w_down):
    normed = rms_norm(x_rows, norm_pre).astype(jnp.bfloat16)
    gathered = lax.all_gather(normed, 'tp', axis=1, tiled=True)
    gate_proj = jnp.einsum('bcd,df->bcf', gathered, w_gate, preferred_element_type=jnp.float32)
    up_proj = jnp.einsum('bcd,df->bcf', gathered, w_up, preferred_element_type=jnp.float32)
    gated = (jax.nn.gelu(gate_proj, approximate=True) * up_proj).astype(jnp.bfloat16)
    part_sum = jnp.einsum('bcf,fd->bcd', gated, w_down, preferred_element_type=jnp.float32).astype(jnp.bfloat16)
    mlp_rows = lax.psum_scatter(part_sum, 'tp', scatter_dimension=1, tiled=True)
    return (x_rows.astype(jnp.float32) + rms_norm(mlp_rows, norm_post)).astype(jnp.bfloat16)


def solution(mesh):
    tp_size = mesh.shape['tp']
    act_spec = P('dp', 'tp', None)
    cache_spec = P('dp', None, 'tp', None)
    col_spec = P(None, None, 'tp')
    row_spec = P(None, 'tp', None)
    arg_specs = (act_spec, P('dp'), cache_spec, cache_spec, cache_spec, cache_spec, P(), col_spec, col_spec, col_spec, row_spec, col_spec, col_spec, row_spec)
    result_specs = (act_spec, cache_spec, cache_spec, cache_spec, cache_spec)

    def device_step(x, start, k_local, v_local, k_global, v_global, norms, w_q, w_k, w_v, w_o, w_gate, w_up, w_down):
        chunk_len = x.shape[1] * tp_size
        positions = start[:, None] + jnp.arange(chunk_len, dtype=jnp.int32)[None, :]
        hidden, k_local_new, v_local_new = attention_half(x, positions, start, k_local, v_local, norms[0, 0], norms[0, 1], w_q[0], w_k[0], w_v[0], w_o[0], True)
        hidden = mlp_half(hidden, norms[0, 2], norms[0, 3], w_gate[0], w_up[0], w_down[0])
        hidden, k_global_new, v_global_new = attention_half(hidden, positions, start, k_global, v_global, norms[1, 0], norms[1, 1], w_q[1], w_k[1], w_v[1], w_o[1], False)
        hidden = mlp_half(hidden, norms[1, 2], norms[1, 3], w_gate[1], w_up[1], w_down[1])
        return (hidden, k_local_new, v_local_new, k_global_new, v_global_new)

    return jax.shard_map(device_step, mesh=mesh, in_specs=arg_specs, out_specs=result_specs, check_vma=False)
```

profile of v0, /device:TPU:81, one launch (start us, length us, event | category | flops | bytes accessed | tf_op | source)
XLA Modules:
  0.0 854.8 jit_solution(3237799916891327662)
XLA Ops:
  7.3 3.3 copy.160
  13.1 5.9 slice_bitcast_fusion.1
  19.0 6.6 copy.43
  27.5 36.6 %all-gather.5.cloned.1.call-done = bf16[2,512,4096]{2,1,0:T(8,128)(2,1)} async-done(((bf16[2,64,4096]{2,1,0:T(8,128)(2,1)}), bf16[2,512,4096]{2,1,0:T(8,128)(2,1)}) %all-gather.5.cloned.1.call-update) | async-done | bytes 8388624 | tf_op jit(solution)/shard_map/all_gather | solution.py:79
  64.1 6.3 convolution_bitcast_fusion.1
  71.8 8.4 fusion.66
  88.1 79.5 %while.69 = (s32[]{:T(128)}, bf16[2,512,512]{2,1,0:T(8,128)(2,1)}, bf16[2,512,4,128]{1,3,2,0:T(8,128)(2,1)}, s32[2,512]{1,0:T(2,128)S(1)}, bf16[2,4608,1,128]{3,...) while((s32[]{:T(128)}, bf16[2,512,512]{2,1,0:T(8,128)(2,1)}, ...), condition=%wide.region_6.7_spmd, body=%wide.region_1.6_spmd.sunk | while | flops 615813184 | bytes 30573108 | solution.py:101
  90.7 35.1 %while.76 = (s32[]{:T(128)}, bf16[8,64,1,4,128]{4,3,1,0,2:T(4,128)(2,1)}, s32[4608]{0:T(1024)S(1)}, s32[8,64]{1,0:T(8,128)S(1)}, bf16[8,64,1,4,128]{4,1,0,3,2:T(...) while((s32[]{:T(128)}, ...), condition=%wide.region_5.5_spmd, body=%wide.region_2.4_spmd.sunk | while | flops 615813184 | bytes 17420124 | solution.py:71
  130.3 35.1 %while.76 = (s32[]{:T(128)}, bf16[8,64,1,4,128]{4,3,1,0,2:T(4,128)(2,1)}, s32[4608]{0:T(1024)S(1)}, s32[8,64]{1,0:T(8,128)S(1)}, bf16[8,64,1,4,128]{4,1,0,3,2:T(...) while((s32[]{:T(128)}, ...), condition=%wide.region_5.5_spmd, body=%wide.region_2.4_spmd.sunk | while | flops 615813184 | bytes 17420124 | solution.py:71
  167.6 10.3 %convolution_convert_fusion.1 = bf16[2,512,4096]{2,1,0:T(8,128)(2,1)} fusion(bf16[2,512,512]{2,1,0:T(8,128)(2,1)} %get-tuple-element.392, bf16[2,512,4096]{2,1,0:T(8,128)(2,1)} %param.34), kind=kOutput, calls=%fused_computation.95 | convolution fusion | flops 4299161600 | bytes 13631488 | tf_op jit(solution)/shard_map/bcn,nd->bcd/dot_general | solution.py:102
  178.0 48.9 %reduce-scatter.5.cloned.1.call-done = bf16[2,64,4096]{2,1,0:T(8,128)(2,1)} async-done(((bf16[2,512,4096]{2,1,0:T(8,128)(2,1)}), bf16[2,64,4096]{2,1,0:T(8,128)(2,1)}) %reduce-scatter.5.cloned.1.call-update) | async-done | bytes 1048592 | tf_op jit(solution)/shard_map/reduce_scatter | solution.py:103
  231.7 47.0 %all-gather.7.cloned.1.call-done = bf16[2,512,4096]{2,1,0:T(8,128)(2,1)} async-done(((bf16[2,64,4096]{2,1,0:T(8,128)(2,1)}), bf16[2,512,4096]{2,1,0:T(8,128)(2,1)}) %all-gather.7.cloned.1.call-update) | async-done | bytes 8388624 | tf_op jit(solution)/shard_map/all_gather | solution.py:110
  278.7 22.2 %fusion.56 = f32[2,512,1792]{2,1,0:T(8,128)} fusion(bf16[2,512,4096]{2,1,0:T(8,128)(2,1)} %all-gather.7.cloned.1.call-done, bf16[2,4096,1792]{2,1,0:T(8,128)(2,1)} %param.35), kind=kOutput, calls=%fused_computation.78 | convolution fusion | flops 15032385536 | bytes 30408704 | tf_op jit(solution)/shard_map/bcd,df->bcf/dot_general | solution.py:111
  301.0 23.3 %fusion.82 = bf16[2,512,1792]{2,1,0:T(8,128)(2,1)} fusion(f32[2,512,1792]{2,1,0:T(8,128)} %fusion.56, bf16[2,512,4096]{2,1,0:T(8,128)(2,1)S(1)} %copy-done.41, bf16[2,4096,1792]{2,1,0:T(8,128)(2,1)} %param.36), kind=kOutput, calls=%fused_computation.104 | convolution fusion | flops 15050735616 | bytes 34078720 | tf_op jit(solution)/shard_map/bcd,df->bcf/dot_general | solution.py:112
  324.3 21.7 %fusion.68 = bf16[2,512,4096]{2,1,0:T(8,128)(2,1)} fusion(bf16[2,512,1792]{2,1,0:T(8,128)(2,1)} %fusion.82, bf16[2,1792,4096]{2,1,0:T(8,128)(2,1)} %param.37), kind=kOutput, calls=%fused_computation.92 | convolution fusion | flops 15036579840 | bytes 26738688 | tf_op jit(solution)/shard_map/bcf,fd->bcd/dot_general | solution.py:114
  346.2 48.8 %reduce-scatter.7.cloned.1.call-done = bf16[2,64,4096]{2,1,0:T(8,128)(2,1)} async-done(((bf16[2,512,4096]{2,1,0:T(8,128)(2,1)}), bf16[2,64,4096]{2,1,0:T(8,128)(2,1)}) %reduce-scatter.7.cloned.1.call-update) | async-done | bytes 1048592 | tf_op jit(solution)/shard_map/reduce_scatter | solution.py:115
  401.7 6.7 copy.48
  408.4 39.5 %all-gather.9.cloned.1.call-done = bf16[2,512,4096]{2,1,0:T(8,128)(2,1)} async-done(((bf16[2,64,4096]{2,1,0:T(8,128)(2,1)}), bf16[2,512,4096]{2,1,0:T(8,128)(2,1)}) %all-gather.9.cloned.1.call-update) | async-done | bytes 8388624 | tf_op jit(solution)/shard_map/all_gather | solution.py:79
  447.9 6.3 convolution_bitcast_fusion
  455.4 19.8 %while.72 = (s32[]{:T(128)}, bf16[2,4608,1,128]{3,1,2,0:T(8,128)(2,1)}, s32[2,4]{1,0:T(2,128)S(1)}, bf16[2,512,1,128]{1,3,0,2:T(8,128)(2,1)S(1)}, s32[]{:T(128)}, /*index=5*/s32[4]{0:T(128)S(1)}, s32[]{:T(128)}) while((s32[]{:T(128)}, bf16[2,4608,1,128]{3,1,2,0:T(8,128)(2,1)}, s32[2,4]{1,0:T(2,128)S(1)}, bf16[2,512,1,128]{1,3,0,2:T(8,128)(2,1)S(1)}, ...), condition=%wide.while_cond.1, body=%wide.while_body.1.sunk | while | flops 65565 | bytes 1179843 | solution.py:47
  456.1 3.3 and_reduce_fusion.4
  459.5 2.9 dynamic-slice_select_fusion.4
  462.4 2.9 dynamic-update-slice.13
  465.9 3.3 and_reduce_fusion.4
  469.3 2.9 dynamic-slice_select_fusion.4
  472.2 3.0 dynamic-update-slice.13
  475.2 6.1 fusion.124
  481.3 15.2 %while.73 = (s32[]{:T(128)}, bf16[2,4608,1,128]{3,1,2,0:T(8,128)(2,1)S(1)}, s32[2,4]{1,0:T(2,128)S(1)}, bf16[2,512,1,128]{3,1,2,0:T(8,128)(2,1)S(1)}, s32[]{:T(128)}, /*index=5*/s32[4]{0:T(128)S(1)}, s32[]{:T(128)}) while((s32[]{:T(128)}, bf16[2,4608,1,128]{3,1,2,0:T(8,128)(2,1)S(1)}, s32[2,4]{1,0:T(2,128)S(1)}, ...), condition=%wide.while_cond.2, body=%wide.while_body.2.sunk | while | flops 65565 | bytes 655555 | solution.py:47
  482.0 3.3 and_reduce_fusion.5
  489.6 3.3 and_reduce_fusion.5
  496.6 8.3 fusion.64
  507.5 107.7 %while.71 = (s32[]{:T(128)}, bf16[2,512,512]{2,1,0:T(8,128)(2,1)}, bf16[2,512,4,128]{1,3,2,0:T(8,128)(2,1)}, s32[2,512]{1,0:T(2,128)S(1)}, bf16[2,4608,1,128]{3,...) while((s32[]{:T(128)}, bf16[2,512,512]{2,1,0:T(8,128)(2,1)}, ...), condition=%wide.region_20.21_spmd, body=%wide.region_15.20_spmd.sunk | while | flops 614923776 | bytes 35263568 | solution.py:101
  507.5 2.9 dynamic-slice_bitcast_fusion.7
  510.9 48.3 %while.77 = (s32[]{:T(128)}, bf16[8,64,1,4,128]{4,3,1,0,2:T(4,128)(2,1)}, s32[4608]{0:T(1024)S(1)}, s32[8,64]{1,0:T(8,128)S(1)}, bf16[8,64,1,4,128]{4,1,0,3,2:T(...) while((s32[]{:T(128)}, ...), condition=%wide.region_19.19_spmd, body=%wide.region_16.18_spmd.sunk | while | flops 614923776 | bytes 22110584 | solution.py:71
  561.2 2.9 dynamic-slice_bitcast_fusion.7
  564.6 48.3 %while.77 = (s32[]{:T(128)}, bf16[8,64,1,4,128]{4,3,1,0,2:T(4,128)(2,1)}, s32[4608]{0:T(1024)S(1)}, s32[8,64]{1,0:T(8,128)S(1)}, bf16[8,64,1,4,128]{4,1,0,3,2:T(...) while((s32[]{:T(128)}, ...), condition=%wide.region_19.19_spmd, body=%wide.region_16.18_spmd.sunk | while | flops 614923776 | bytes 22110584 | solution.py:71
  615.2 11.2 %convolution_convert_fusion = bf16[2,512,4096]{2,1,0:T(8,128)(2,1)} fusion(bf16[2,512,512]{2,1,0:T(8,128)(2,1)} %get-tuple-element.393, bf16[2,512,4096]{2,1,0:T(8,128)(2,1)} %param.34), kind=kOutput, calls=%fused_computation.94 | convolution fusion | flops 4299161600 | bytes 13631488 | tf_op jit(solution)/shard_map/bcn,nd->bcd/dot_general | solution.py:102
  626.5 48.8 %reduce-scatter.9.cloned.1.call-done = bf16[2,64,4096]{2,1,0:T(8,128)(2,1)} async-done(((bf16[2,512,4096]{2,1,0:T(8,128)(2,1)}), bf16[2,64,4096]{2,1,0:T(8,128)(2,1)}) %reduce-scatter.9.cloned.1.call-update) | async-done | bytes 1048592 | tf_op jit(solution)/shard_map/reduce_scatter | solution.py:103
  680.3 47.0 %all-gather.11.cloned.1.call-done = bf16[2,512,4096]{2,1,0:T(8,128)(2,1)} async-done(((bf16[2,64,4096]{2,1,0:T(8,128)(2,1)}), bf16[2,512,4096]{2,1,0:T(8,128)(2,1)}) %all-gather.11.cloned.1.call-update) | async-done | bytes 8388624 | tf_op jit(solution)/shard_map/all_gather | solution.py:110
  727.3 21.8 %fusion.50 = f32[2,512,1792]{2,1,0:T(8,128)} fusion(bf16[2,512,4096]{2,1,0:T(8,128)(2,1)} %all-gather.11.cloned.1.call-done, bf16[2,4096,1792]{2,1,0:T(8,128)(2,1)} %param.35), kind=kOutput, calls=%fused_computation.72 | convolution fusion | flops 15032385536 | bytes 30408704 | tf_op jit(solution)/shard_map/bcd,df->bcf/dot_general | solution.py:111
  749.0 23.4 %fusion.91 = bf16[2,512,1792]{2,1,0:T(8,128)(2,1)} fusion(f32[2,512,1792]{2,1,0:T(8,128)} %fusion.50, bf16[2,512,4096]{2,1,0:T(8,128)(2,1)S(1)} %copy-done.42, bf16[2,4096,1792]{2,1,0:T(8,128)(2,1)} %param.36), kind=kOutput, calls=%fused_computation.113 | convolution fusion | flops 15050735616 | bytes 34078720 | tf_op jit(solution)/shard_map/bcd,df->bcf/dot_general | solution.py:112
  772.4 21.8 %fusion.71 = bf16[2,512,4096]{2,1,0:T(8,128)(2,1)} fusion(bf16[2,512,1792]{2,1,0:T(8,128)(2,1)} %fusion.91, bf16[2,1792,4096]{2,1,0:T(8,128)(2,1)} %param.37), kind=kOutput, calls=%fused_computation.93 | convolution fusion | flops 15036579840 | bytes 26738688 | tf_op jit(solution)/shard_map/bcf,fd->bcd/dot_general | solution.py:114
  800.8 6.9 while.75
  801.4 2.9 bitcast_dynamic-update-slice_fusion.2
  804.8 2.9 bitcast_dynamic-update-slice_fusion.2
  809.7 10.3 %while.74 = (s32[]{:T(128)}, bf16[2,8192,1,128]{1,3,0,2:T(8,128)(2,1)}, s32[2,4]{1,0:T(2,128)S(1)}, bf16[2,4096,1,128]{3,1,2,0:T(8,128)(2,1)}, s32[]{:T(128)}) while((s32[]{:T(128)}, bf16[2,8192,1,128]{1,3,0,2:T(8,128)(2,1)}, s32[2,4]{1,0:T(2,128)S(1)}, bf16[2,4096,1,128]{3,1,2,0:T(8,128)(2,1)}, s32[]{:T(128)}) %tuple.267), condition=%wide.while_cond, body=%wide.while_body.sunk | while | flops 2 | bytes 6292089 | solution.py:40
  820.0 6.2 broadcast_select_fusion
  826.2 17.1 %reduce-scatter.11.cloned.1.call-done = bf16[2,64,4096]{2,1,0:T(8,128)(2,1)} async-done(((bf16[2,512,4096]{2,1,0:T(8,128)(2,1)}), bf16[2,64,4096]{2,1,0:T(8,128)(2,1)}) %reduce-scatter.11.cloned.1.call-update) | async-done | bytes 1048592 | tf_op jit(solution)/shard_map/reduce_scatter | solution.py:115
  (469 shorter events, 248.2 us)
Async XLA Ops:
  7.2 4.2 copy-start.5
  7.2 3.4 copy-start.22
  7.2 56.9 %all-gather.5.cloned.1.call-start = ((), (), s32[]{:S(2)}) async-start(), calls=%async_computation.4 | async-start | bytes 9437184 | tf_op jit(solution)/shard_map/all_gather | solution.py:79
  13.0 213.8 %reduce-scatter.5.cloned.1.call-start = ((), (), s32[]{:S(2)}) async-start(), calls=%async_computation.5 | async-start | bytes 9437184 | tf_op jit(solution)/shard_map/reduce_scatter | solution.py:103
  19.0 6.6 copy-start.34
  19.0 45.1 %copy-start.18 = (bf16[2,4096,128]{2,1,0:T(8,128)(2,1)S(1)}, bf16[2,4096,128]{2,1,0:T(8,128)(2,1)}, u32[]{:S(2)}) copy-start(bf16[2,4096,128]{2,1,0:T(8,128)(2,1)} %param.32) | copy-start | bytes 6291460
  25.7 44.7 %copy-start.36 = (f32[64]{0:T(128)}, f32[64]{0:T(128)S(1)}, u32[]{:S(2)}) copy-start(f32[64]{0:T(128)S(1)} %multiply_power_fusion) | copy-start | bytes 772
  26.4 44.1 %copy-start.23 = (f32[2,512]{1,0:T(2,128)}, f32[2,512]{1,0:T(2,128)S(1)}, u32[]{:S(2)}) copy-start(f32[2,512]{1,0:T(2,128)S(1)} %get-tuple-element.644) | copy-start | bytes 12292
  27.3 52.9 %copy-start.12 = (f32[2,512,64]{1,2,0:T(8,128)}, f32[2,512,64]{1,2,0:T(8,128)S(1)}, u32[]{:S(2)}) copy-start(f32[2,512,64]{1,2,0:T(8,128)S(1)} %get-tuple-element.636) | copy-start | bytes 786436
  27.4 52.9 %copy-start.14 = (f32[2,512,64]{1,2,0:T(8,128)}, f32[2,512,64]{1,2,0:T(8,128)S(1)}, u32[]{:S(2)}) copy-start(f32[2,512,64]{1,2,0:T(8,128)S(1)} %get-tuple-element.637) | copy-start | bytes 786436
  71.6 8.6 %copy-start.16 = (bf16[2,512,1,128]{1,3,0,2:T(8,128)(2,1)}, bf16[2,512,1,128]{1,3,0,2:T(8,128)(2,1)S(1)}, u32[]{:S(2)}) copy-start(bf16[2,512,1,128]{1,3,0,2:T(8,128)(2,1)S(1)} %pad_maximum_fusion.6) | copy-start | bytes 786436
  71.8 9.9 %slice-start = ((s8[8388608]{0:T(1024)(128)(4,1)}), s8[4194304]{0:T(1024)(128)(4,1)S(1)}, s32[]{:S(2)}) async-start(s8[8388608]{0:T(1024)(128)(4,1)} %bitcast.311), calls=%async_computation.12 | async-start | bytes 8388608
  71.8 9.9 %slice-start.1 = ((s8[8388608]{0:T(1024)(128)(4,1)}), s8[4194304]{0:T(1024)(128)(4,1)S(1)}, s32[]{:S(2)}) async-start(s8[8388608]{0:T(1024)(128)(4,1)} %bitcast.311), calls=%async_computation.13 | async-start | bytes 8388608
  82.2 2.3 copy-start.10
  82.2 2.4 copy-start.11
  84.5 2.5 copy-start.20
  88.3 1.9 copy-start.3
  177.8 50.5 %copy-start.6 = (bf16[2,64,4096]{2,1,0:T(8,128)(2,1)S(1)}, bf16[2,64,4096]{2,1,0:T(8,128)(2,1)}, u32[]{:S(2)}) copy-start(bf16[2,64,4096]{2,1,0:T(8,128)(2,1)} %param.24) | copy-start | bytes 3145732
  177.8 50.5 %copy-start.31 = (f32[1,1,4096]{2,1,0:T(1,128)S(1)}, f32[1,1,4096]{2,1,0:T(1,128)}, u32[]{:S(2)}) copy-start(f32[1,1,4096]{2,1,0:T(1,128)} %get-tuple-element.631) | copy-start | bytes 49156
  177.9 52.4 %copy-start.30 = (f32[1,1,4096]{2,1,0:T(1,128)S(1)}, f32[1,1,4096]{2,1,0:T(1,128)}, u32[]{:S(2)}) copy-start(f32[1,1,4096]{2,1,0:T(1,128)} %get-tuple-element.630) | copy-start | bytes 49156
  177.9 100.8 %all-gather.7.cloned.1.call-start = ((), (), s32[]{:S(2)}) async-start(), calls=%async_computation.6 | async-start | bytes 9437184 | tf_op jit(solution)/shard_map/all_gather | solution.py:110
  231.7 163.3 %reduce-scatter.7.cloned.1.call-start = ((), (), s32[]{:S(2)}) async-start(), calls=%async_computation.7 | async-start | bytes 9437184 | tf_op jit(solution)/shard_map/reduce_scatter | solution.py:115
  278.7 22.2 %copy-start.41 = (bf16[2,512,4096]{2,1,0:T(8,128)(2,1)S(1)}, bf16[2,512,4096]{2,1,0:T(8,128)(2,1)}, u32[]{:S(2)}) copy-start(bf16[2,512,4096]{2,1,0:T(8,128)(2,1)} %all-gather.7.cloned.1.call-done) | copy-start | bytes 25165828
  346.0 50.5 %copy-start.29 = (f32[1,1,4096]{2,1,0:T(1,128)S(1)}, f32[1,1,4096]{2,1,0:T(1,128)}, u32[]{:S(2)}) copy-start(f32[1,1,4096]{2,1,0:T(1,128)} %get-tuple-element.629) | copy-start | bytes 49156
  346.0 53.4 %copy-start.28 = (f32[1,1,4096]{2,1,0:T(1,128)S(1)}, f32[1,1,4096]{2,1,0:T(1,128)}, u32[]{:S(2)}) copy-start(f32[1,1,4096]{2,1,0:T(1,128)} %get-tuple-element.628) | copy-start | bytes 49156
  346.0 54.8 %copy-start.39 = (s32[2,1]{0,1:T(1,128)S(1)}, s32[2,1]{0,1:T(1,128)}, u32[]{:S(2)}) copy-start(s32[2,1]{0,1:T(1,128)} %get-tuple-element.642) | copy-start | bytes 28
  346.1 54.8 %copy-start.40 = (s32[3]{0:T(128)S(1)}, s32[3]{0:T(128)}, u32[]{:S(2)}) copy-start(s32[3]{0:T(128)} %constant.262.clone.1) | copy-start | bytes 40
  346.1 54.9 %copy-start.38 = (s32[2,1]{0,1:T(1,128)S(1)}, s32[2,1]{0,1:T(1,128)}, u32[]{:S(2)}) copy-start(s32[2,1]{0,1:T(1,128)} %get-tuple-element.640) | copy-start | bytes 28
  346.1 101.8 %all-gather.9.cloned.1.call-start = ((), (), s32[]{:S(2)}) async-start(), calls=%async_computation.8 | async-start | bytes 9437184 | tf_op jit(solution)/shard_map/all_gather | solution.py:79
  400.8 274.5 %reduce-scatter.9.cloned.1.call-start = ((), (), s32[]{:S(2)}) async-start(), calls=%async_computation.9 | async-start | bytes 9437184 | tf_op jit(solution)/shard_map/reduce_scatter | solution.py:103
  401.7 46.2 %copy-start.19 = (bf16[2,4096,128]{2,1,0:T(8,128)(2,1)S(1)}, bf16[2,4096,128]{2,1,0:T(8,128)(2,1)}, u32[]{:S(2)}) copy-start(bf16[2,4096,128]{2,1,0:T(8,128)(2,1)} %param.32) | copy-start | bytes 6291460
  408.4 45.8 %copy-start.24 = (f32[2,512]{1,0:T(2,128)S(1)}, f32[2,512]{1,0:T(2,128)}, u32[]{:S(2)}) copy-start(f32[2,512]{1,0:T(2,128)} %copy-done.23) | copy-start | bytes 12292
  408.4 45.8 %copy-start.37 = (f32[64]{0:T(128)S(1)}, f32[64]{0:T(128)}, u32[]{:S(2)}) copy-start(f32[64]{0:T(128)} %copy-done.36) | copy-start | bytes 772
  408.4 47.0 %copy-start.32 = (s32[4]{0:T(128)S(1)}, s32[4]{0:T(128)}, u32[]{:S(2)}) copy-start(s32[4]{0:T(128)} %constant.509) | copy-start | bytes 52
  475.2 6.1 copy-start.1
  496.6 8.4 copy-start.13
  496.6 8.4 copy-start.15
  507.5 2.9 copy-start.4
  561.2 2.9 copy-start.4
  615.1 11.2 %copy-start = (bf16[2,4608,1,128]{3,1,2,0:T(8,128)(2,1)}, bf16[2,4608,1,128]{3,1,2,0:T(8,128)(2,1)S(1)}, u32[]{:S(2)}) copy-start(bf16[2,4608,1,128]{3,1,2,0:T(8,128)(2,1)S(1)} %get-tuple-element.1185) | copy-start | bytes 7077892
  626.3 50.5 %copy-start.8 = (bf16[2,64,4096]{2,1,0:T(8,128)(2,1)S(1)}, bf16[2,64,4096]{2,1,0:T(8,128)(2,1)}, u32[]{:S(2)}) copy-start(bf16[2,64,4096]{2,1,0:T(8,128)(2,1)} %copy-done.7) | copy-start | bytes 3145732
  626.3 50.5 %copy-start.27 = (f32[1,1,4096]{2,1,0:T(1,128)S(1)}, f32[1,1,4096]{2,1,0:T(1,128)}, u32[]{:S(2)}) copy-start(f32[1,1,4096]{2,1,0:T(1,128)} %get-tuple-element.627) | copy-start | bytes 49156
  626.4 52.4 %copy-start.26 = (f32[1,1,4096]{2,1,0:T(1,128)S(1)}, f32[1,1,4096]{2,1,0:T(1,128)}, u32[]{:S(2)}) copy-start(f32[1,1,4096]{2,1,0:T(1,128)} %get-tuple-element.633) | copy-start | bytes 49156
  626.4 100.8 %all-gather.11.cloned.1.call-start = ((), (), s32[]{:S(2)}) async-start(), calls=%async_computation.10 | async-start | bytes 9437184 | tf_op jit(solution)/shard_map/all_gather | solution.py:110
  680.2 163.1 %reduce-scatter.11.cloned.1.call-start = ((), (), s32[]{:S(2)}) async-start(), calls=%async_computation.11 | async-start | bytes 9437184 | tf_op jit(solution)/shard_map/reduce_scatter | solution.py:115
  727.3 21.8 %copy-start.42 = (bf16[2,512,4096]{2,1,0:T(8,128)(2,1)S(1)}, bf16[2,512,4096]{2,1,0:T(8,128)(2,1)}, u32[]{:S(2)}) copy-start(bf16[2,512,4096]{2,1,0:T(8,128)(2,1)} %all-gather.11.cloned.1.call-done) | copy-start | bytes 25165828
  807.7 2.0 copy-start.9
  820.0 24.8 %copy-start.25 = (f32[1,1,4096]{2,1,0:T(1,128)S(1)}, f32[1,1,4096]{2,1,0:T(1,128)}, u32[]{:S(2)}) copy-start(f32[1,1,4096]{2,1,0:T(1,128)} %get-tuple-element.626) | copy-start | bytes 49156
  (23 other events, 28.8 us)
Sparse Core Ops, SparseCore 0:
  13.1 50.9 all-gather.4
  178.0 48.7 reduce-scatter.4
  231.8 46.8 all-gather.6
  346.2 48.7 reduce-scatter.6
  400.9 46.9 all-gather.8
  626.5 48.7 reduce-scatter.8
  680.3 46.9 all-gather.10
  794.5 48.7 reduce-scatter.10
where the time goes:
time: 865 us; the launch traced here: 855 us
  waiting for transfers between devices  334 us (39%)
  matrix products  295 us (34%)
  local copies, waits for them, and re-layouts  109 us (13%)
  other arithmetic  99.3 us (11%)
  between operations  15.2 us (2%)
    reduce_scatter x2, waiting for transfers between devices, attention_half(): lax.psum_scatter(part_sum, 'tp', scatter_dimension=1, tiled=True)  97.7 us
    all_gather x2, waiting for transfers between devices, mlp_half(): gathered = lax.all_gather(normed, 'tp', axis=1, tiled=True)  94 us
    all_gather x2, waiting for transfers between devices, attention_half(): gathered = lax.all_gather(normed, 'tp', axis=1, tiled=True)  76.1 us
    reduce_scatter x2, waiting for transfers between devices, mlp_half(): mlp_rows = lax.psum_scatter(part_sum, 'tp', scatter_dimension=1, tiled=True)  65.9 us
    dot_general x32, matrix products, one_block(): jnp.einsum('qkgd,tkd->kgqt', q_blk, k_seq, preferred_element_type=jnp.flo...  65.3 us
    dot_general x2, matrix products, mlp_half(): jnp.einsum('bcd,df->bcf', gathered, w_up, preferred_element_type=jnp.floa...  46.7 us
    dot_general x2, matrix products, mlp_half(): jnp.einsum('bcd,df->bcf', gathered, w_gate, preferred_element_type=jnp.fl...  44 us
    dot_general x2, matrix products, mlp_half(): jnp.einsum('bcf,fd->bcd', gated, w_down, preferred_element_type=jnp.float32)  43.6 us
  transfers between devices with their start and end apart: 8, of which 8 were waited for; matrix products, arithmetic and copies ran while one was open for 6% of the time, Pallas kernels for 0%

commit v1 on v0

v1 whole, which is shorter than its diff:
```python
import jax
import jax.numpy as jnp
import numpy as np
from jax import lax
from jax.experimental import pallas as pl
from jax.experimental.pallas import tpu as pltpu
from jax.sharding import PartitionSpec as P

SOFT_CAP = 50.0
NORM_EPS = 1e-6
ROPE_BASE = 10000.0
MASKED = -1e30
DIST = 2
LOWEST = -3e38
LOG2E = 1.4426950408889634

BF16 = jnp.bfloat16
F32 = jnp.float32
MESH_ID = pl.DeviceIdType.MESH
ANY = pl.BlockSpec(memory_space=pl.ANY)
VMEM = pl.BlockSpec(memory_space=pltpu.VMEM)
SMEM = pl.BlockSpec(memory_space=pltpu.SMEM)

TILE = 256
SLOTS = 4
DOWN = 2
QROWS = 256
KEYS = 512
OUT = 512
VMEM_LIMIT = 67_000_000
ATT_PLAN = (0, 4, 6, 11, 13, 15, 17, 20, 25)
MLP_PLAN = (0, 2, 3, 5, 6, 8, 10, 12, 14)
SWAP_ORDER = (2, 1, 3, 0)
DO_COMPUTE = True
DO_COMM = True

RS_RIGHT = ((2, 0), (1, 1), (1, 0))
RS_LEFT = ((2, 1), (3, 0), (3, 1))
AG_RIGHT = ((0, 0), (0, 1), (3, 0))
AG_LEFT = ((0, 1), (0, 0), (1, 1))
AG_FROM_LEFT = ((3, 0), (3, 1), (2, 0))
AG_FROM_RIGHT = ((1, 1), (1, 0), (2, 1))


def dot(a, b):
    return jnp.dot(a, b, preferred_element_type=F32)


def dot_nt(a, b):
    return lax.dot_general(a, b, (((1,), (1,)), ((), ())), preferred_element_type=F32)


def layers_kernel(x_hbm, start_ref, freq_ref, norms_ref, kl_hbm, vl_hbm, kg_hbm, vg_hbm,
                  wq_hbm, wk_hbm, wv_hbm, wo_hbm, wg_hbm, wu_hbm, wd_hbm,
                  xo_hbm, kn_hbm, vn_hbm,
                  g, y, rb, ring_l, ring_r, xs, cos_ref, sin_ref, bias, wqkv, wo, slots, h_sc, q_sc, o_sc, kbuf, vbuf, t_sc, mx_sc,
                  s_x, s_attw, s_slot, s_kv, s_kvo, s_xo,
                  rs_ds, rs_dr, rs_rl, rs_rr, rs_sr, ag_sr, ag_rl, ag_rr, ag_ds, ag_dr):
    chunk, dim = g.shape[1], g.shape[2]
    rows = xs.shape[1]
    half = rows // 2
    piece = rows // 4
    hd = kbuf.shape[2]
    past = kbuf.shape[1] - chunk
    n_q = wq_hbm.shape[2] // TILE
    heads = wq_hbm.shape[2] // hd
    ffn = wg_hbm.shape[2]
    n_up = ffn // TILE
    n_down = dim // TILE
    per_phase = 2 * n_up + n_down
    n_tiles = 4 * per_phase
    n_blocks = heads * chunk // QROWS
    per_head = chunk // QROWS
    c1 = (hd ** -0.5) / SOFT_CAP
    c2 = SOFT_CAP * LOG2E

    dp = lax.axis_index('dp')
    me = lax.axis_index('tp')
    chip = me // 2
    core = me % 2
    right = (dp, ((chip + 1) % 4) * 2 + core)
    left = (dp, ((chip + 3) % 4) * 2 + core)
    sibling = (dp, chip * 2 + 1 - core)

    def base(offset, c):
        return ((chip + offset) % 4 * 2 + c) * rows

    def span(start, size):
        return pl.ds(pl.multiple_of(start, 16), size)

    def push(src, dst, ssem, rsem, dev):
        return pltpu.make_async_remote_copy(src_ref=src, dst_ref=dst, send_sem=ssem, recv_sem=rsem, device_id=dev, device_id_type=MESH_ID)

    def att_weight_copies(l):
        out = [pltpu.make_async_copy(wq_hbm.at[l, :, pl.ds(i * TILE, TILE)], wqkv.at[i], s_attw.at[i]) for i in range(n_q)]
        out.append(pltpu.make_async_copy(wk_hbm.at[l], wqkv.at[n_q, :, pl.ds(0, hd)], s_attw.at[n_q]))
        out.append(pltpu.make_async_copy(wv_hbm.at[l], wqkv.at[n_q, :, pl.ds(hd, hd)], s_attw.at[n_q + 1]))
        out.append(pltpu.make_async_copy(wo_hbm.at[l], wo, s_attw.at[n_q + 2]))
        return out

    def cache_copies(k_hbm, v_hbm, s):
        return [pltpu.make_async_copy(k_hbm.at[s, pl.ds(0, past)], kbuf.at[s, pl.ds(0, past)], s_kv.at[s, 0]),
                pltpu.make_async_copy(v_hbm.at[s, pl.ds(0, past)], vbuf.at[s, pl.ds(0, past)], s_kv.at[s, 1])]

    def start_tile(m):
        layer = m // (2 * per_phase)
        j = m % per_phase
        slot = m % SLOTS

        @pl.when((j < 2 * n_up) & (j % 2 == 0))
        def _():
            pltpu.make_async_copy(wg_hbm.at[layer, :, pl.ds(pl.multiple_of(j // 2 * TILE, TILE), TILE)], slots.at[slot], s_slot.at[slot]).start()

        @pl.when((j < 2 * n_up) & (j % 2 == 1))
        def _():
            pltpu.make_async_copy(wu_hbm.at[layer, :, pl.ds(pl.multiple_of(j // 2 * TILE, TILE), TILE)], slots.at[slot], s_slot.at[slot]).start()

        @pl.when(j >= 2 * n_up)
        def _():
            pltpu.make_async_copy(wd_hbm.at[layer, :, pl.ds(pl.multiple_of((j - 2 * n_up) * TILE, TILE), TILE)],
                                  slots.at[slot, pl.ds(0, ffn)], s_slot.at[slot]).start()

    def next_tile(m):
        @pl.when(m + SLOTS < n_tiles)
        def _():
            start_tile(m + SLOTS)

    def wait_up_tile(slot):
        pltpu.make_async_copy(wg_hbm.at[0, :, pl.ds(0, TILE)], slots.at[slot], s_slot.at[slot]).wait()

    def wait_down_tile(slot):
        pltpu.make_async_copy(wd_hbm.at[0, :, pl.ds(0, TILE)], slots.at[slot, pl.ds(0, ffn)], s_slot.at[slot]).wait()

    def swap(s, r, cols):
        return push(y.at[s, span(base(r, 1 - core), rows), cols], rb.at[s, r, :, cols], rs_ds.at[s, r], rs_dr.at[s, r], sibling)

    def swap_columns(s, first, size):
        if DO_COMM:
            for r in SWAP_ORDER:
                swap(s, r, pl.ds(pl.multiple_of(first, TILE), size)).start()

    def swapped(s, r):
        return swap(s, r, pl.ds(0, dim))

    def rs_right(s, u, k):
        r, hh = RS_RIGHT[k]
        src = y.at[s, span(base(r, core) + u * half + hh * piece, piece)]
        return push(src, ring_l.at[s, u, k], rs_sr.at[s, u, 0, k], rs_rl.at[s, u, k], right)

    def rs_left(s, u, k):
        r, hh = RS_LEFT[k]
        src = y.at[s, span(base(r, core) + u * half + hh * piece, piece)]
        return push(src, ring_r.at[s, u, k], rs_sr.at[s, u, 1, k], rs_rr.at[s, u, k], left)

    def add_in(s, row0, n, src):
        step = min(1024, dim)

        def body(i, carry):
            cols = pl.ds(pl.multiple_of(i * step, step), step)
            total = y[s, span(row0, n), cols].astype(F32) + src[:, cols].astype(F32)
            y[s, span(row0, n), cols] = total.astype(BF16)
            return carry

        lax.fori_loop(0, dim // step, body, 0)

    def fold(s, u, r):
        if u == 0:
            swapped(s, r).wait_recv()
        add_in(s, base(r, core) + u * half, half, rb.at[s, r, span(u * half, half)])

    def rs1(s, u):
        fold(s, u, 2)
        rs_right(s, u, 0).start()
        rs_left(s, u, 0).start()

    def rs2(s, u):
        fold(s, u, 1)
        rs_right(s, u, 1).start()
        fold(s, u, 3)
        rs_left(s, u, 1).start()

    def rs3(s, u):
        rs_right(s, u, 0).wait_recv()
        add_in(s, base(1, core) + u * half, piece, ring_l.at[s, u, 0])
        rs_right(s, u, 2).start()
        rs_left(s, u, 0).wait_recv()
        add_in(s, base(3, core) + u * half + piece, piece, ring_r.at[s, u, 0])
        rs_left(s, u, 2).start()

    def rs4_wait(s, u):
        if u == 0:
            swapped(s, 0).wait_recv()
        for k in (1, 2):
            rs_right(s, u, k).wait_recv()
            rs_left(s, u, k).wait_recv()

    def rs_drain(s):
        for r in range(4):
            swapped(s, r).wait_send()
        for u in range(2):
            for k in range(3):
                rs_right(s, u, k).wait_send()
                rs_left(s, u, k).wait_send()

    def norm_row(i):
        return norms_ref[i // 4, pl.ds(i % 4, 1)]

    def inv_rms(v):
        return lax.rsqrt(jnp.sum(v * v, axis=-1, keepdims=True) * (1.0 / dim) + NORM_EPS)

    def finish(s, u, post, has_next):
        def body(hh, carry):
            row0 = u * half + hh * piece
            loc = span(row0, piece)
            total = (y[s, span(base(0, core) + row0, piece)].astype(F32) + rb[s, 0, loc].astype(F32)
                     + ring_l[s, u, 2 - hh].astype(F32) + ring_r[s, u, 1 + hh].astype(F32))
            v = total.astype(BF16).astype(F32)
            x1 = (xs[s, loc].astype(F32) + v * inv_rms(v) * (1.0 + norm_row(post))).astype(BF16)
            xs[s, loc] = x1
            if has_next:
                w = x1.astype(F32)
                a = w * inv_rms(w) * (1.0 + norm_row(post + 1))
                g[s, span(base(0, core) + row0, piece)] = a.astype(BF16)
            return carry

        lax.fori_loop(0, 2, body, 0)

    def ag_piece(t, u, where):
        r, hh = where
        return g.at[t, span(base(r, core) + u * half + hh * piece, piece)]

    def ag_right(t, u, k, table=AG_RIGHT):
        ref = ag_piece(t, u, table[k])
        return push(ref, ref, ag_sr.at[t, u, 0, k], ag_rl.at[t, u, k], right)

    def ag_left(t, u, k, table=AG_LEFT):
        ref = ag_piece(t, u, table[k])
        return push(ref, ref, ag_sr.at[t, u, 1, k], ag_rr.at[t, u, k], left)

    def from_left(t, u, k):
        ag_right(t, u, k, AG_FROM_LEFT).wait_recv()

    def from_right(t, u, k):
        ag_left(t, u, k, AG_FROM_RIGHT).wait_recv()

    def ag_d2d(t, u, r):
        ref = g.at[t, span(base(r, core) + u * half, half)]
        return push(ref, ref, ag_ds.at[t, u, r], ag_dr.at[t, u, r], sibling)

    def ag1(t, u):
        for k in range(2):
            ag_right(t, u, k).start()
            ag_left(t, u, k).start()
        ag_d2d(t, u, 0).start()

    def ag2(t, u):
        from_left(t, u, 0)
        ag_right(t, u, 2).start()
        from_right(t, u, 0)
        ag_left(t, u, 2).start()

    def ag3(t, u):
        from_left(t, u, 1)
        ag_d2d(t, u, 3).start()
        from_right(t, u, 1)
        ag_d2d(t, u, 1).start()

    def ag4(t, u):
        from_left(t, u, 2)
        from_right(t, u, 2)
        ag_d2d(t, u, 2).start()

    def ag5(t):
        for u in range(2):
            for r in range(4):
                ref = g.at[t, span(base(r, 1 - core) + u * half, half)]
                push(ref, ref, ag_ds.at[t, u, r], ag_dr.at[t, u, r], sibling).wait_recv()

    def ag_drain(t):
        for u in range(2):
            for k in range(3):
                ag_right(t, u, k).wait_send()
                ag_left(t, u, k).wait_send()
            for r in range(4):
                ag_d2d(t, u, r).wait_send()

    def rope(v, s):
        return v * cos_ref[s] + pltpu.roll(v, hd // 2, 1) * sin_ref[s]

    def project_q(i, s):
        p = dot(g[s], wqkv[i])
        for hh in range(TILE // hd):
            rot = rope(p[:, hh * hd:(hh + 1) * hd], s).astype(BF16)
            for b in range(per_head):
                q_sc[(i * (TILE // hd) + hh) * per_head + b] = rot[b * QROWS:(b + 1) * QROWS]

    def project_kv(s):
        p = dot(g[s], wqkv[n_q])
        kbuf[s, pl.ds(past, chunk)] = rope(p[:, :hd], s).astype(BF16)
        vbuf[s, pl.ds(past, chunk)] = p[:, hd:].astype(BF16)

    def fresh_out(s, l):
        return [pltpu.make_async_copy(kbuf.at[s, pl.ds(past, chunk)], kn_hbm.at[l, s], s_kvo.at[0]),
                pltpu.make_async_copy(vbuf.at[s, pl.ds(past, chunk)], vn_hbm.at[l, s], s_kvo.at[1])]

    def scores(b, s, l):
        tok = (b % per_head) * QROWS
        diff = lax.broadcasted_iota(jnp.int32, (QROWS, KEYS), 1) - lax.broadcasted_iota(jnp.int32, (QROWS, KEYS), 0)
        oldest = jnp.where(l == 0, start_ref[s] - past, -past) + tok
        q = q_sc[b]
        top = None
        for kb in range((past + chunk) // KEYS):
            first = kb * KEYS
            cols = pl.ds(first, KEYS)
            t = jnp.tanh(dot_nt(q, kbuf[s, cols]) * c1)
            if past // 2 <= first < past:
                t = t + bias[s, :, cols]
            if first < chunk:
                t = jnp.where(diff > oldest - first, t, MASKED)
            if first >= past:
                t = jnp.where(diff <= tok - (first - past), t, MASKED)
            t_sc[:, cols] = t
            for i in range(KEYS // hd):
                ti = t[:, i * hd:(i + 1) * hd]
                top = ti if top is None else jnp.maximum(top, ti)
        mx_sc[...] = top

    def weigh(b, s):
        mc = jnp.max(mx_sc[...], axis=-1, keepdims=True) * c2
        mc = jnp.broadcast_to(mc, (QROWS, hd))
        n_kb = (past + chunk) // KEYS
        total = acc = None
        pvs = []
        for kb in range(n_kb):
            cols = pl.ds(kb * KEYS, KEYS)
            if kb >= DIST:
                mc = jnp.maximum(mc, jnp.minimum(pvs[kb - DIST], LOWEST))
            ps = []
            for i in range(KEYS // hd):
                pi = jnp.exp2(t_sc[:, pl.ds(kb * KEYS + i * hd, hd)] * c2 - mc)
                total = pi if total is None else total + pi
                ps.append(pi.astype(BF16))
            pv = dot(jnp.concatenate(ps, axis=1), vbuf[s, cols])
            pvs.append(pv)
            acc = pv if acc is None else acc + pv
        o = acc / jnp.sum(total, axis=-1, keepdims=True)
        o_sc[pl.ds(pl.multiple_of((b % per_head) * QROWS, QROWS), QROWS), pl.ds(pl.multiple_of(b // per_head * hd, hd), hd)] = o.astype(BF16)

    def out_tile(i, s):
        step = min(OUT, dim)
        cols = pl.ds(pl.multiple_of(i * step, step), step)
        y[s, :, cols] = dot(o_sc[...], wo[:, cols]).astype(BF16)

    def up_tile(jj, s, m0):
        m = m0 + 2 * jj
        sa, sb = m % SLOTS, (m + 1) % SLOTS
        wait_up_tile(sa)
        wait_up_tile(sb)
        gate = dot(g[s], slots[sa])
        up = dot(g[s], slots[sb])
        h_sc[:, pl.ds(pl.multiple_of(jj * TILE, TILE), TILE)] = (jax.nn.gelu(gate, approximate=True) * up).astype(BF16)
        next_tile(m)
        next_tile(m + 1)

    def down_tiles(n, s, m0):
        m = m0 + 2 * n_up + DOWN * n
        for i in range(DOWN):
            wait_down_tile((m + i) % SLOTS)
        for i in range(DOWN):
            cols = pl.ds(pl.multiple_of((DOWN * n + i) * TILE, TILE), TILE)
            y[s, :, cols] = dot(h_sc[...], slots[(m + i) % SLOTS, pl.ds(0, ffn)]).astype(BF16)
        for i in range(DOWN):
            next_tile(m + i)

    def events(t, post, reduce, gather):
        def reduced(u):
            @pl.when(reduce)
            def _():
                rs4_wait(t, u)

                @pl.when(gather)
                def _():
                    finish(t, u, post, True)
                    ag1(t, u)

                @pl.when(jnp.logical_not(gather))
                def _():
                    finish(t, u, post, False)

        def if_reduce(*what):
            def run():
                @pl.when(reduce)
                def _():
                    for f, u in what:
                        f(t, u)
            return run

        def if_gather(f, u):
            return lambda: pl.when(gather)(lambda: f(t, u))

        return (if_reduce((rs3, 0), (rs2, 1)), if_reduce((rs3, 1)), lambda: reduced(0), lambda: reduced(1),
                if_gather(ag2, 0), if_gather(ag3, 0), if_gather(ag2, 1), if_gather(ag3, 1), if_gather(ag4, 0))

    def at(step, low, high, plan, todo):
        if DO_COMM:
            for when, what in zip(plan, todo):
                if low <= when < high:
                    pl.when(step == when)(what)

    def tail(s, t, plan, todo, last, reduce, gather):
        if DO_COMM:
            for when, what in zip(plan, todo):
                if when >= last:
                    what()
            for u in range(2):
                rs1(s, u)
                if u == 0:
                    rs2(s, u)

            @pl.when(gather)
            def _():
                ag4(t, 1)
                ag5(t)
                ag_drain(t)
            pl.when(reduce)(lambda: rs_drain(t))

    def att_phase(l, s):
        t = 1 - s
        reduce = (l > 0) | (s > 0)
        todo = events(t, 4 * l - 1 + 2 * s, reduce, l >= 0)
        step = min(OUT, dim)
        first_block = n_q + 1
        first_out = first_block + 2 * n_blocks
        last = first_out + dim // step
        plan = ATT_PLAN
        if DO_COMPUTE:
            for c in att_weight_copies(l)[:-1]:
                pl.when(s == 0)(c.wait)

        def proj(i, carry):
            if DO_COMPUTE:
                project_q(i, s)
            at(i, 0, n_q, plan, todo)
            return carry

        lax.fori_loop(0, n_q, proj, 0)
        if DO_COMPUTE:
            project_kv(s)
            for c in fresh_out(s, l):
                c.start()
            for c in cache_copies(kl_hbm, vl_hbm, s):
                c.wait()
        at(n_q, n_q, first_block, plan, todo)

        def blk(i, carry):
            if DO_COMPUTE:
                pl.when(i % 2 == 0)(lambda: scores(i // 2, s, l))
                pl.when(i % 2 == 1)(lambda: weigh(i // 2, s))
            at(first_block + i, first_block, first_out, plan, todo)
            return carry

        lax.fori_loop(0, 2 * n_blocks, blk, 0)
        if DO_COMPUTE:
            @pl.when(l == 0)
            def _():
                for c in cache_copies(kg_hbm, vg_hbm, s):
                    c.start()
            pl.when(s == 0)(att_weight_copies(l)[-1].wait)

        def out_body(i, carry):
            if DO_COMPUTE:
                out_tile(i, s)
            swap_columns(s, i * step, step)
            at(first_out + i, first_out, last, plan, todo)
            return carry

        lax.fori_loop(0, dim // step, out_body, 0)
        if DO_COMPUTE:
            @pl.when((s == 1) & (l == 0))
            def _():
                for c in att_weight_copies(1):
                    c.start()
            for c in fresh_out(s, l):
                c.wait()
        tail(s, t, plan, todo, last, reduce, l >= 0)

    def mlp_phase(l, s):
        t = 1 - s
        m0 = (2 * l + s) * per_phase
        gather = (l == 0) | (s == 0)
        todo = events(t, 4 * l + 1 + 2 * s, l >= 0, gather)
        last = n_up + n_down // DOWN
        plan = MLP_PLAN

        def ups(jj, carry):
            if DO_COMPUTE:
                up_tile(jj, s, m0)
            at(jj, 0, n_up, plan, todo)
            return carry

        lax.fori_loop(0, n_up, ups, 0)

        def downs(n, carry):
            if DO_COMPUTE:
                down_tiles(n, s, m0)
            swap_columns(s, n * (DOWN * TILE), DOWN * TILE)
            at(n_up + n, n_up, last, plan, todo)
            return carry

        lax.fori_loop(0, last - n_up, downs, 0)
        tail(s, t, plan, todo, last, l >= 0, gather)

    xcopy = pltpu.make_async_copy(x_hbm, xs, s_x)
    xcopy.start()
    barrier = pltpu.get_barrier_semaphore()
    for dev in (sibling, left, right):
        pl.semaphore_signal(barrier, inc=1, device_id=dev, device_id_type=MESH_ID)

    def first_norm(s):
        def body(k, carry):
            v = xs[s, span(k * piece, piece)].astype(F32)
            a = v * inv_rms(v) * (1.0 + norm_row(0))
            g[s, span(base(0, core) + k * piece, piece)] = a.astype(BF16)
            return carry

        lax.fori_loop(0, 4, body, 0)

    xcopy.wait()
    first_norm(0)
    pl.semaphore_wait(barrier, 3)
    if DO_COMM:
        for u in range(2):
            ag1(0, u)
    if DO_COMPUTE:
        for c in att_weight_copies(0):
            c.start()
        for s in range(2):
            for c in cache_copies(kl_hbm, vl_hbm, s):
                c.start()
        for m in range(SLOTS):
            start_tile(jnp.int32(m))
    first_norm(1)
    for s in range(2):
        pos = (lax.broadcasted_iota(jnp.int32, (chunk, hd), 0) + start_ref[s]).astype(F32)
        angle = pos * freq_ref[...]
        low = lax.broadcasted_iota(jnp.int32, (chunk, hd), 1) < hd // 2
        cos_ref[s] = jnp.cos(angle)
        sin = jnp.sin(angle)
        sin_ref[s] = jnp.where(low, -sin, sin)
        bias[s] = jnp.where(lax.broadcasted_iota(jnp.int32, (1, past), 1) < start_ref[s], 0.0, MASKED)
    if DO_COMM:
        for u in range(2):
            ag2(0, u)
        for u in range(2):
            ag1(1, u)
        for u in range(2):
            ag3(0, u)
        for u in range(2):
            ag4(0, u)
        ag5(0)
        ag_drain(0)

    def layer(l, carry):
        def att(s, carry):
            att_phase(l, s)
            return carry

        def mlp(s, carry):
            mlp_phase(l, s)
            return carry

        lax.fori_loop(0, 2, att, 0)
        lax.fori_loop(0, 2, mlp, 0)
        return carry

    lax.fori_loop(0, 2, layer, 0)

    out0 = pltpu.make_async_copy(xs.at[0], xo_hbm.at[0], s_xo.at[0])
    out0.start()
    if DO_COMM:
        rs3(1, 0)
        rs2(1, 1)
        rs3(1, 1)

        for u in range(2):
            rs4_wait(1, u)
            finish(1, u, 7, False)
        rs_drain(1)
    out1 = pltpu.make_async_copy(xs.at[1], xo_hbm.at[1], s_xo.at[1])
    out1.start()
    out0.wait()
    out1.wait()


def run_layers(x, start, freq, norms, kl, vl, kg, vg, wq, wk, wv, wo, wg, wu, wd):
    seqs, rows, dim = x.shape
    past, hd = kl.shape[1], kl.shape[2]
    chunk = kg.shape[1] - past
    n_q = wq.shape[2] // TILE
    ring = pltpu.VMEM((2, 2, 3, rows // 4, dim), BF16)
    keys = pltpu.VMEM((2, past + chunk, hd), BF16)
    whole = pltpu.VMEM((2, chunk, dim), BF16)
    table = pltpu.VMEM((2, chunk, hd), F32)

    def dmas(*shape):
        return pltpu.SemaphoreType.DMA(shape)

    scratch = [
        whole, whole,
        pltpu.VMEM((2, 4, rows, dim), BF16),
        ring, ring,
        pltpu.VMEM((2, rows, dim), BF16),
        table, table,
        pltpu.VMEM((2, 1, past), F32),
        pltpu.VMEM((n_q + 1, dim, TILE), BF16),
        pltpu.VMEM(wo.shape[1:], BF16),
        pltpu.VMEM((SLOTS, max(dim, wd.shape[1]), TILE), BF16),
        pltpu.VMEM((chunk, wg.shape[2]), BF16),
        pltpu.VMEM((wq.shape[2] // hd * chunk // QROWS, QROWS, hd), BF16),
        pltpu.VMEM((chunk, wq.shape[2]), BF16),
        keys, keys,
        pltpu.VMEM((QROWS, past + chunk), F32),
        pltpu.VMEM((QROWS, hd), F32),
        pltpu.SemaphoreType.DMA, dmas(n_q + 3), dmas(SLOTS), dmas(2, 2), dmas(2), dmas(2),
    ]
    chips = [dmas(2, 2, 3)] * 2
    cores = [dmas(2, 2, 4)] * 2
    swaps = [dmas(2, 4)] * 2
    sends = [dmas(2, 2, 2, 3)]
    scratch += swaps + chips + sends + sends + chips + cores
    return pl.pallas_call(
        layers_kernel,
        out_shape=(jax.ShapeDtypeStruct(x.shape, BF16),) + (jax.ShapeDtypeStruct((2, seqs, chunk, hd), BF16),) * 2,
        in_specs=[ANY, SMEM, VMEM, VMEM] + [ANY] * 11,
        out_specs=(ANY,) * 3,
        scratch_shapes=scratch,
        compiler_params=pltpu.CompilerParams(collective_id=0, has_side_effects=True, vmem_limit_bytes=VMEM_LIMIT),
        name='layers',
    )(x, start, freq, norms, kl, vl, kg, vg, wq, wk, wv, wo, wg, wu, wd)


def cache_kernel(start_ref, x, k_new, v_new, kl, vl, kg, vg, x_o, kl_o, vl_o, kg_o, vg_o, xbuf, buf, fresh, s_x, s_in, s_fr, s_out):
    chunk = k_new.shape[2]
    window = kl.shape[1]
    lead = fresh.shape[1] - chunk
    n_buf = buf.shape[0]
    jobs = []
    for b in range(kl.shape[0]):
        for l, pairs in enumerate((((kl, k_new, kl_o), (vl, v_new, vl_o)), ((kg, k_new, kg_o), (vg, v_new, vg_o)))):
            jobs += [(src, new, dst, l, b) for src, new, dst in pairs]

    def load(i):
        src, new, _, l, b = jobs[i]
        k = i % n_buf
        return (pltpu.make_async_copy(src.at[b], buf.at[k, pl.ds(0, src.shape[1])], s_in.at[k]),
                pltpu.make_async_copy(new.at[l, b], fresh.at[k, pl.ds(0, chunk)], s_fr.at[k]))

    def store(i):
        src, _, dst, _, b = jobs[i]
        k = i % n_buf
        return pltpu.make_async_copy(buf.at[k, pl.ds(0, src.shape[1])], dst.at[b], s_out.at[k])

    x_in = pltpu.make_async_copy(x, xbuf, s_x)
    x_out = pltpu.make_async_copy(xbuf, x_o, s_x)
    x_in.start()
    for i in range(n_buf):
        for c in load(i):
            c.start()
    x_in.wait()
    x_out.start()
    for i, (_, _, _, l, b) in enumerate(jobs):
        k = i % n_buf
        for c in load(i):
            c.wait()
        start = start_ref[b]
        r = start % lead
        at = pl.multiple_of(start - r, lead)
        rolled = pltpu.roll(fresh[k].astype(F32), r, 0)
        row = lax.broadcasted_iota(jnp.int32, rolled.shape, 0)
        old = buf[k, pl.ds(at, chunk + lead)].astype(F32)
        buf[k, pl.ds(at, chunk + lead)] = jnp.where((row >= r) & (row < r + chunk), rolled, old).astype(BF16)
        if l == 0:
            over = buf[k, pl.ds(window, chunk)].astype(F32)
            row = lax.broadcasted_iota(jnp.int32, over.shape, 0)
            head = buf[k, pl.ds(0, chunk)].astype(F32)
            buf[k, pl.ds(0, chunk)] = jnp.where(row < start + chunk - window, over, head).astype(BF16)
        store(i).start()
        if i >= 1 and i - 1 + n_buf < len(jobs):
            store(i - 1).wait()
            for c in load(i - 1 + n_buf):
                c.start()
    for i in range(max(0, len(jobs) - n_buf), len(jobs)):
        store(i).wait()
    x_out.wait()


def write_caches(start, x, k_new, v_new, kl, vl, kg, vg):
    hd = kl.shape[2]
    chunk = k_new.shape[2]
    lead = 16
    depth = max(kl.shape[1] + chunk, kg.shape[1]) + lead
    n_buf = 8
    dmas = pltpu.SemaphoreType.DMA((n_buf,))
    return pl.pallas_call(
        cache_kernel,
        out_shape=tuple(jax.ShapeDtypeStruct(c.shape, BF16) for c in (x, kl, vl, kg, vg)),
        in_specs=[SMEM] + [ANY] * 7,
        out_specs=(ANY,) * 5,
        scratch_shapes=[pltpu.VMEM(x.shape, BF16), pltpu.VMEM((n_buf, depth, hd), BF16), pltpu.VMEM((n_buf, chunk + lead, hd), BF16),
                        pltpu.SemaphoreType.DMA, dmas, dmas, dmas],
        compiler_params=pltpu.CompilerParams(vmem_limit_bytes=VMEM_LIMIT),
        name='write_caches',
    )(start, x, k_new, v_new, kl, vl, kg, vg)


def solution(mesh):
    act_spec = P('dp', 'tp', None)
    cache_spec = P('dp', None, 'tp', None)
    col_spec = P(None, None, 'tp')
    row_spec = P(None, 'tp', None)
    arg_specs = (act_spec, P('dp'), cache_spec, cache_spec, cache_spec, cache_spec, P(), col_spec, col_spec, col_spec, row_spec, col_spec, col_spec, row_spec)
    result_specs = (act_spec, cache_spec, cache_spec, cache_spec, cache_spec)

    def device_step(x, start, k_local, v_local, k_global, v_global, norms, w_q, w_k, w_v, w_o, w_gate, w_up, w_down):
        hd = k_local.shape[3]
        freq = ROPE_BASE ** (np.arange(hd // 2) * (-2.0 / hd))
        freq = jnp.asarray(np.concatenate([freq, freq])[None], F32)
        flat = [c.reshape(c.shape[0], c.shape[1], hd) for c in (k_local, v_local, k_global, v_global)]
        x_out, k_new, v_new = run_layers(x, start, freq, norms, *flat, w_q, w_k, w_v, w_o, w_gate, w_up, w_down)
        x_out, *caches = write_caches(start, x_out, k_new, v_new, *flat)
        return (x_out,) + tuple(c.reshape(c.shape[0], c.shape[1], 1, hd) for c in caches)

    return jax.shard_map(device_step, mesh=mesh, in_specs=arg_specs, out_specs=result_specs, check_vma=False)
```

time: 865 us -> 328 us (0.38); the launches traced: 855 us -> 328 us
  waiting for transfers between devices: 334 us -> 0 us
  Pallas kernels: 0 us -> 327 us
  matrix products: 295 us -> 0 us
  local copies, waits for them, and re-layouts: 109 us -> 0 us
  other arithmetic: 99.3 us -> 0 us
  between operations: 15.2 us -> 0.82 us
    pallas_call x0 -> x2, Pallas kernels: none -> 327 us  [the longest x1 319 us: run_layers(): pl.pallas_call(layers_kernel, out_shape=(jax.ShapeDtypeStruct(x.shape, BF...]
    dot_general x78 -> x0, matrix products: 295 us -> none  [the longest x32 65.3 us: one_block(): jnp.einsum('qkgd,tkd->kgqt', q_blk, k_seq, preferred_element_type=jnp.flo...]
    all_gather x4 -> x0, waiting for transfers between devices: 170 us -> none  [the longest x2 94 us: mlp_half(): gathered = lax.all_gather(normed, 'tp', axis=1, tiled=True)]
    reduce_scatter x4 -> x0, waiting for transfers between devices: 164 us -> none  [the longest x2 97.7 us: attention_half(): lax.psum_scatter(part_sum, 'tp', scatter_dimension=1, tiled=True)]
    reduce_sum x40 -> x0, other arithmetic: 37.4 us -> none  [the longest x32 25.2 us: one_block(): jnp.sum(weights, axis=-1, keepdims=True)]
    dynamic_update_slice x36 -> x0, local copies, waits for them, and re-layouts: 25.3 us -> none  [the longest x32 22 us: attend_seq(): all_blocks = lax.map(one_block, (q_blocks, pos_blocks))]
    scatter x8 -> x0, other arithmetic: 22.8 us -> none
    another operation x21 -> x0, local copies, waits for them, and re-layouts: 21.5 us -> none  [the longest x19 19.4 us: window_write(): jnp.roll(rows, amount, axis=0)]
  transfers between devices with their start and end apart: 8 -> 0, of which waited for: 8 -> 0; matrix products, arithmetic and copies ran while one was open for 6% -> 0% of each run, Pallas kernels for 0% -> 0%
where the time goes in v1:
time: 328 us
  Pallas kernels  327 us (100%)
    pallas_call x1, Pallas kernels, run_layers(): pl.pallas_call(layers_kernel, out_shape=(jax.ShapeDtypeStruct(x.shape, BF...  319 us
    pallas_call x1, Pallas kernels, write_caches(): pl.pallas_call(cache_kernel, out_shape=tuple((jax.ShapeDtypeStruct(c.shap...  8.44 us

profile of v1, /device:TPU:81, one launch (start us, length us, event | category | flops | bytes accessed | tf_op | source)
XLA Modules:
  0.0 328.1 jit_solution(8505743346980371541)
XLA Ops:
  0.6 318.8 %layers.1 = (bf16[2,64,4096]{2,1,0:T(8,128)(2,1)}, bf16[2,2,512,128]{3,2,1,0:T(8,128)(2,1)}, bf16[2,2,512,128]{3,2,1,0:T(8,128)(2,1)}) custom-call(bf16[2,64,4096]{2,1,0:T(8,128)(2,1)} %x_hbm.1, s32[2]{0:T(128)} %start_ref.3, f32[1,128]{1,0:T(1,128)} %constant.2.clone.freq_ref, f32[2,4,4096]{2,1,0:T(4,128)} %norms_ref.1, bf16[2,4096,128]{2,1,0:T(8,128)(2,1)} %bitcast.20, ...), custom_call_target="tpu_custom_call" | custom-call | tf_op jit(solution)/shard_map/layers/pallas_call | solution.py:631
  319.5 8.4 %write_caches.1 = (bf16[2,64,4096]{2,1,0:T(8,128)(2,1)}, bf16[2,4096,128]{2,1,0:T(8,128)(2,1)}, bf16[2,4096,128]{2,1,0:T(8,128)(2,1)}, bf16[2,4608,128]{2,1,0:T(8,128)(2,1)}, bf16[2,4608,128]{2,1,0:T(8,128)(2,1)}) custom-call(s32[2]{0:T(128)} %start_ref.3, bf16[2,64,4096]{2,1,0:T(8,128)(2,1)} %get-tuple-element.13.x, ...), custom_call_target="tpu_custom_call" | custom-call | tf_op jit(solution)/shard_map/write_caches/pallas_call | solution.py:704

commit v2 on v1

v2 whole, which is shorter than its diff:
```python
import jax
import jax.numpy as jnp
import numpy as np
from jax import lax
from jax.experimental import pallas as pl
from jax.experimental.pallas import tpu as pltpu
from jax.sharding import PartitionSpec as P

SOFT_CAP = 50.0
NORM_EPS = 1e-6
ROPE_BASE = 10000.0
MASKED = -1e30
DIST = 2
LOWEST = -3e38
LOG2E = 1.4426950408889634

BF16 = jnp.bfloat16
F32 = jnp.float32
MESH_ID = pl.DeviceIdType.MESH
ANY = pl.BlockSpec(memory_space=pl.ANY)
VMEM = pl.BlockSpec(memory_space=pltpu.VMEM)
SMEM = pl.BlockSpec(memory_space=pltpu.SMEM)

TILE = 256
SLOTS = 5
DOWN = 2
QROWS = 256
KEYS = 512
OUT = 2048
VMEM_LIMIT = 67_000_000
LAYERS_LIMIT = 67_000_000
SWAP = 1024
ATT_PLAN = (4, 10, 12, 16, 19, 21, 22, 23, 24)
MLP_PLAN = (2, 5, 6, 8, 10, 11, 13, 15, 16)
LAST_RS3 = 7
SWAP_ORDER = (2, 1, 3, 0)
DO_COMPUTE = True
DO_COMM = True

PAIR = range(2)

RS_RIGHT = ((2, 0), (1, 1), (1, 0))
RS_LEFT = ((2, 1), (3, 0), (3, 1))
AG_RIGHT = ((0, 0), (0, 1), (3, 0))
AG_LEFT = ((0, 1), (0, 0), (1, 1))
AG_FROM_LEFT = ((3, 0), (3, 1), (2, 0))
AG_FROM_RIGHT = ((1, 1), (1, 0), (2, 1))


def repeat(n, body, low=0):
    lax.fori_loop(low, n, body, 0)


def dot(a, b):
    return jnp.dot(a, b, preferred_element_type=F32)


def dot_nt(a, b):
    return lax.dot_general(a, b, (((1,), (1,)), ((), ())), preferred_element_type=F32)


def layers_kernel(x_hbm, start_ref, freq_ref, norms_ref, kl_hbm, vl_hbm, kg_hbm, vg_hbm,
                  wq_hbm, wk_hbm, wv_hbm, wo_hbm, wg_hbm, wu_hbm, wd_hbm,
                  xo_hbm, kn_hbm, vn_hbm,
                  g, y, rb, ring_l, ring_r, xs, cos_ref, sin_ref, bias, wqkv, wo, slots, h_sc, q_sc, o_sc, kbuf, vbuf, t_sc, mx_sc,
                  s_x, s_attw, s_slot, s_kv, s_kvo, s_xo, credit,
                  rs_ds, rs_dr, rs_rl, rs_rr, rs_sr, ag_sr, ag_rl, ag_rr, ag_ds, ag_dr):
    devices, half, dim = g.shape[1], g.shape[3], g.shape[4]
    chunk = devices * 2 * half
    piece = half // 2
    hd = kbuf.shape[1]
    past = kbuf.shape[0] - chunk
    n_q = wq_hbm.shape[2] // TILE
    heads = wq_hbm.shape[2] // hd
    ffn = wg_hbm.shape[2]
    n_up = ffn // TILE
    n_down = dim // TILE
    n_pairs = n_down // DOWN
    per_phase = 2 * n_up + n_pairs
    n_tiles = 4 * per_phase + n_pairs
    n_blocks = heads * chunk // QROWS
    per_head = chunk // QROWS
    owners = devices // per_head
    c1 = (hd ** -0.5) / SOFT_CAP
    c2 = SOFT_CAP * LOG2E

    dp = lax.axis_index('dp')
    me = lax.axis_index('tp')
    chip = me // 2
    core = me % 2
    chips = devices // 2
    right = (dp, (chip + 1) % chips * 2 + core)
    left = (dp, (chip + chips - 1) % chips * 2 + core)
    sibling = (dp, chip * 2 + 1 - core)
    partners = (sibling, left, right)

    def owner(offset, c):
        return (chip + offset) % chips * 2 + c

    def columns(first, size):
        return pl.ds(pl.multiple_of(first, TILE), size)

    def rows(hh):
        return pl.ds(pl.multiple_of(hh * piece, piece), piece)

    def push(src, dst, ssem, rsem, dev):
        return pltpu.make_async_remote_copy(src_ref=src, dst_ref=dst, send_sem=ssem, recv_sem=rsem, device_id=dev, device_id_type=MESH_ID)

    def att_weight_copies(l):
        out = [pltpu.make_async_copy(wq_hbm.at[l, :, pl.ds(i * TILE, TILE)], wqkv.at[i], s_attw.at[i]) for i in range(n_q)]
        out.append(pltpu.make_async_copy(wk_hbm.at[l], wqkv.at[n_q, :, pl.ds(0, hd)], s_attw.at[n_q]))
        out.append(pltpu.make_async_copy(wv_hbm.at[l], wqkv.at[n_q, :, pl.ds(hd, hd)], s_attw.at[n_q + 1]))
        out.append(pltpu.make_async_copy(wo_hbm.at[l], wo, s_attw.at[n_q + 2]))
        return out

    def cache_copies(k_hbm, v_hbm, s):
        return [pltpu.make_async_copy(c.at[s, pl.ds(0, past)], buf.at[pl.ds(0, past)], s_kv.at[i])
                for i, (c, buf) in enumerate(((k_hbm, kbuf), (v_hbm, vbuf)))]

    def start_tile(m):
        slot = m % SLOTS
        m = jnp.where(m < n_tiles - n_pairs, m, m - n_pairs)
        layer = m // (2 * per_phase)
        j = m % per_phase

        @pl.when((j < 2 * n_up) & (j % 2 == 0))
        def _():
            pltpu.make_async_copy(wg_hbm.at[layer, :, columns(j // 2 * TILE, TILE)], slots.at[slot, pl.ds(0, dim)], s_slot.at[slot, 0]).start()

        @pl.when((j < 2 * n_up) & (j % 2 == 1))
        def _():
            pltpu.make_async_copy(wu_hbm.at[layer, :, columns(j // 2 * TILE, TILE)], slots.at[slot, pl.ds(0, dim)], s_slot.at[slot, 0]).start()

        @pl.when(j >= 2 * n_up)
        def _():
            for i in range(DOWN):
                pltpu.make_async_copy(wd_hbm.at[layer, :, columns(((j - 2 * n_up) * DOWN + i) * TILE, TILE)],
                                      slots.at[slot, pl.ds(i * ffn, ffn)], s_slot.at[slot, i]).start()

    def next_tile(m):
        @pl.when(m + SLOTS < n_tiles)
        def _():
            start_tile(m + SLOTS)

    def wait_up_tile(slot):
        pltpu.make_async_copy(wg_hbm.at[0, :, pl.ds(0, TILE)], slots.at[slot, pl.ds(0, dim)], s_slot.at[slot, 0]).wait()

    def wait_down_pair(slot):
        for i in range(DOWN):
            pltpu.make_async_copy(wd_hbm.at[0, :, pl.ds(0, TILE)], slots.at[slot, pl.ds(i * ffn, ffn)], s_slot.at[slot, i]).wait()

    def swap(s, u, r, cols):
        which, i = (slice(None), 0) if u is None else (u, u)
        return push(y.at[s, owner(r, 1 - core), which, :, cols], rb.at[r, which, :, cols], rs_ds.at[s, i, r], rs_dr.at[s, i, r], sibling)

    def swap_columns(s, u, first, size):
        if DO_COMM:
            for r in SWAP_ORDER:
                swap(s, u, r, columns(first, size)).start()

    def swapped(s, u, r):
        return swap(s, u, r, pl.ds(0, dim))

    def rs_right(s, u, k):
        r, hh = RS_RIGHT[k]
        return push(y.at[s, owner(r, core), u, rows(hh)], ring_l.at[u, k], rs_sr.at[s, u, 0, k], rs_rl.at[s, u, k], right)

    def rs_left(s, u, k):
        r, hh = RS_LEFT[k]
        return push(y.at[s, owner(r, core), u, rows(hh)], ring_r.at[u, k], rs_sr.at[s, u, 1, k], rs_rr.at[s, u, k], left)

    def add_in(dst, src):
        step = min(1024, dim)

        def body(i, carry):
            cols = pl.ds(pl.multiple_of(i * step, step), step)
            dst[:, cols] = (dst[:, cols].astype(F32) + src[:, cols].astype(F32)).astype(BF16)
            return carry

        repeat(dim // step, body)

    def fold(s, u, r, apart):
        if apart:
            swapped(s, u, r).wait_recv()
        elif u == 0:
            swapped(s, None, r).wait_recv()
        add_in(y.at[s, owner(r, core), u], rb.at[r, u])

    def rs1(s, u, apart=False):
        fold(s, u, 2, apart)
        rs_right(s, u, 0).start()
        rs_left(s, u, 0).start()

    def rs2(s, u, apart=False):
        hold = apart and u == 1
        fold(s, u, 1, apart)
        if not hold:
            rs_right(s, u, 1).start()
        fold(s, u, 3, apart)
        if hold:
            rs_gone(s, u, 0)
            rs_right(s, u, 1).start()
        rs_left(s, u, 1).start()

    def rs3(s, u):
        rs_right(s, u, 0).wait_recv()
        add_in(y.at[s, owner(1, core), u, rows(0)], ring_l.at[u, 0])
        rs_right(s, u, 2).start()
        rs_left(s, u, 0).wait_recv()
        add_in(y.at[s, owner(3, core), u, rows(1)], ring_r.at[u, 0])
        rs_left(s, u, 2).start()

    def rs4_wait(s, u, apart=False):
        if apart:
            swapped(s, u, 0).wait_recv()
        elif u == 0:
            swapped(s, None, 0).wait_recv()
        for k in (1, 2):
            rs_right(s, u, k).wait_recv()
            rs_left(s, u, k).wait_recv()

    def rs_gone(s, u, k):
        rs_right(s, u, k).wait_send()
        rs_left(s, u, k).wait_send()

    def rs_drain(s, halves=(None,)):
        for u in halves:
            for r in range(4):
                swapped(s, u, r).wait_send()
        for u in PAIR:
            for k in range(3):
                if None in halves or u == 0 or k > 0:
                    rs_gone(s, u, k)

    def norm_row(i):
        return norms_ref[i // 4, pl.ds(i % 4, 1)]

    def inv_rms(v):
        return lax.rsqrt(jnp.sum(v * v, axis=-1, keepdims=True) * (1.0 / dim) + NORM_EPS)

    def finish(s, u, post, has_next):
        def body(hh, carry):
            at = rows(hh)
            total = (y[s, me, u, at].astype(F32) + rb[0, u, at].astype(F32)
                     + ring_l[u, 2 - hh].astype(F32) + ring_r[u, 1 + hh].astype(F32))
            v = total.astype(BF16).astype(F32)
            x1 = (xs[s, u, at].astype(F32) + v * inv_rms(v) * (1.0 + norm_row(post))).astype(BF16)
            xs[s, u, at] = x1
            if has_next:
                w = x1.astype(F32)
                g[s, me, u, at] = (w * inv_rms(w) * (1.0 + norm_row(post + 1))).astype(BF16)
            return carry

        repeat(2, body)

    def ag_right(t, u, k, table=AG_RIGHT):
        r, hh = table[k]
        ref = g.at[t, owner(r, core), u, rows(hh)]
        return push(ref, ref, ag_sr.at[t, u, 0, k], ag_rl.at[t, u, k], right)

    def ag_left(t, u, k, table=AG_LEFT):
        r, hh = table[k]
        ref = g.at[t, owner(r, core), u, rows(hh)]
        return push(ref, ref, ag_sr.at[t, u, 1, k], ag_rr.at[t, u, k], left)

    def from_left(t, u, k):
        ag_right(t, u, k, AG_FROM_LEFT).wait_recv()

    def from_right(t, u, k):
        ag_left(t, u, k, AG_FROM_RIGHT).wait_recv()

    def ag_d2d(t, u, r, c):
        ref = g.at[t, owner(r, c), u]
        return push(ref, ref, ag_ds.at[t, u, r], ag_dr.at[t, u, r], sibling)

    def ag_out(t, u, k):
        ag_right(t, u, k).start()
        ag_left(t, u, k).start()

    def ag_gone(t, u, k):
        ag_right(t, u, k).wait_send()
        ag_left(t, u, k).wait_send()

    def ag1(t, u):
        for k in PAIR:
            ag_out(t, u, k)
        ag_d2d(t, u, 0, core).start()

    def ag2(t, u):
        from_left(t, u, 0)
        ag_right(t, u, 2).start()
        from_right(t, u, 0)
        ag_left(t, u, 2).start()

    def ag3(t, u):
        from_left(t, u, 1)
        ag_d2d(t, u, 3, core).start()
        from_right(t, u, 1)
        ag_d2d(t, u, 1, core).start()

    def ag4(t, u):
        from_left(t, u, 2)
        from_right(t, u, 2)
        ag_d2d(t, u, 2, core).start()

    def ag_own(t):
        for u in PAIR:
            ag_d2d(t, u, 0, 1 - core).wait_recv()

    def ag5(t, u):
        for r in (1, 3, 2):
            ag_d2d(t, u, r, 1 - core).wait_recv()

    def ag_drain(t, first):
        for u in PAIR:
            pl.when(jnp.logical_not(first))(lambda: ag_gone(t, u, 0))
            for k in (1, 2):
                ag_gone(t, u, k)
            for r in range(4):
                ag_d2d(t, u, r, core).wait_send()

    def rows_of(v):
        return v.reshape(chunk // 2, v.shape[-1])

    def rope(v, s, u):
        return v * rows_of(cos_ref[s, :, u]) + pltpu.roll(v, hd // 2, 1) * rows_of(sin_ref[s, :, u])

    def project_q(i, u, s):
        p = dot(rows_of(g[s, :, u]), wqkv[i])
        for hh in range(TILE // hd):
            rot = rope(p[:, hh * hd:(hh + 1) * hd], s, u).astype(BF16)
            q_sc[i * (TILE // hd) + hh, :, u] = rot.reshape(devices, half, hd)

    def project_kv(u, s):
        p = dot(rows_of(g[s, :, u]), wqkv[n_q])
        k = rope(p[:, :hd], s, u).astype(BF16).reshape(devices, half, hd)
        v = p[:, hd:].astype(BF16).reshape(devices, half, hd)
        for j in range(devices):
            at = pl.ds(past + (2 * j + u) * half, half)
            kbuf[at] = k[j]
            vbuf[at] = v[j]

    def fresh_out(s, l):
        return [pltpu.make_async_copy(buf.at[pl.ds(past, chunk)], out.at[l, s], s_kvo.at[i])
                for i, (buf, out) in enumerate(((kbuf, kn_hbm), (vbuf, vn_hbm)))]

    def scores(b, s, l):
        tok = (b % per_head) * QROWS
        diff = lax.broadcasted_iota(jnp.int32, (QROWS, KEYS), 1) - lax.broadcasted_iota(jnp.int32, (QROWS, KEYS), 0)
        oldest = jnp.where(l == 0, start_ref[s] - past, -past) + tok
        q = q_sc[b // per_head, pl.ds(b % per_head * owners, owners)].reshape(QROWS, hd)
        top = None
        for kb in range((past + chunk) // KEYS):
            first = kb * KEYS
            cols = pl.ds(first, KEYS)
            t = jnp.tanh(dot_nt(q, kbuf[cols]) * c1)
            if past // 2 <= first < past:
                t = t + bias[s, :, cols]
            if first < chunk:
                t = jnp.where(diff > oldest - first, t, MASKED)
            if first >= past:
                t = jnp.where(diff <= tok - (first - past), t, MASKED)
            t_sc[:, cols] = t
            for i in range(KEYS // hd):
                ti = t[:, i * hd:(i + 1) * hd]
                top = ti if top is None else jnp.maximum(top, ti)
        mx_sc[...] = top

    def weigh(b, s):
        mc = jnp.max(mx_sc[...], axis=-1, keepdims=True) * c2
        mc = jnp.broadcast_to(mc, (QROWS, hd))
        n_kb = (past + chunk) // KEYS
        total = acc = None
        pvs = []
        for kb in range(n_kb):
            cols = pl.ds(kb * KEYS, KEYS)
            if kb >= DIST:
                mc = jnp.maximum(mc, jnp.minimum(pvs[kb - DIST], LOWEST))
            ps = []
            for i in range(KEYS // hd):
                pi = jnp.exp2(t_sc[:, pl.ds(kb * KEYS + i * hd, hd)] * c2 - mc)
                total = pi if total is None else total + pi
                ps.append(pi.astype(BF16))
            pv = dot(jnp.concatenate(ps, axis=1), vbuf[cols])
            pvs.append(pv)
            acc = pv if acc is None else acc + pv
        o = acc / jnp.sum(total, axis=-1, keepdims=True)
        o_sc[pl.ds(pl.multiple_of((b % per_head) * QROWS, QROWS), QROWS), pl.ds(pl.multiple_of(b // per_head * hd, hd), hd)] = o.astype(BF16)

    def out_tile(i, s):
        step = min(OUT, dim)
        cols = columns(i * step, step)
        y[s, :, :, :, cols] = dot(o_sc[...], wo[:, cols]).astype(BF16).reshape(devices, 2, half, step)

    def gated(x, sa, sb):
        return (jax.nn.gelu(dot(x, slots[sa, pl.ds(0, dim)]), approximate=True) * dot(x, slots[sb, pl.ds(0, dim)])).astype(BF16)

    def up_half(jj, u, s, m0):
        m = m0 + 2 * jj
        h_sc[:, u, :, columns(jj * TILE, TILE)] = gated(rows_of(g[s, :, u]), m % SLOTS, (m + 1) % SLOTS).reshape(devices, half, TILE)

    def up_tile(jj, s, m0):
        m = m0 + 2 * jj
        wait_up_tile(m % SLOTS)
        wait_up_tile((m + 1) % SLOTS)
        h = gated(g[s].reshape(chunk, dim), m % SLOTS, (m + 1) % SLOTS)
        h_sc[:, :, :, columns(jj * TILE, TILE)] = h.reshape(devices, 2, half, TILE)
        next_tile(m)
        next_tile(m + 1)

    def down_pair(n, s, m0, u=None):
        m = m0 + 2 * n_up + n
        slot = m % SLOTS
        wait_down_pair(slot)
        for i in range(DOWN):
            cols = columns((n % n_pairs * DOWN + i) * TILE, TILE)
            w = slots[slot, pl.ds(i * ffn, ffn)]
            if u is None:
                y[s, :, :, :, cols] = dot(h_sc[...].reshape(chunk, ffn), w).astype(BF16).reshape(devices, 2, half, TILE)
            else:
                y[s, :, u, :, cols] = dot(rows_of(h_sc[:, u]), w).astype(BF16).reshape(devices, half, TILE)
        next_tile(m)

    def events(t, post, reduce, gather):
        def reduced(u):
            @pl.when(reduce)
            def _():
                rs4_wait(t, u)

                @pl.when(gather)
                def _():
                    finish(t, u, post, True)
                    ag1(t, u)

                @pl.when(jnp.logical_not(gather))
                def _():
                    finish(t, u, post, False)

        def if_reduce(*what):
            def run():
                @pl.when(reduce)
                def _():
                    for f, u in what:
                        f(t, u)
            return run

        def if_gather(f, u):
            return lambda: pl.when(gather)(lambda: f(t, u))

        return (if_reduce((rs3, 0), (rs2, 1)), if_reduce((rs3, 1)), lambda: reduced(0), lambda: reduced(1),
                if_gather(ag2, 0), if_gather(ag3, 0), if_gather(ag2, 1), if_gather(ag3, 1), if_gather(ag4, 0))

    def at(step, low, high, plan, todo):
        if DO_COMM:
            for when, what in zip(plan, todo):
                if low <= when < high:
                    pl.when(step == when)(what)

    def leave(s):
        rs1(s, 0)
        rs2(s, 0)
        rs1(s, 1)

    def rest(plan, todo, last):
        if DO_COMM:
            for when, what in zip(plan, todo):
                if when >= last:
                    what()

    def att_phase(l, s):
        t = 1 - s
        reduce = (l > 0) | (s > 0)
        todo = events(t, 4 * l - 1 + 2 * s, reduce, l >= 0)
        step = min(OUT, dim)
        swap_step = min(SWAP, dim)
        n_proj = n_q + 1
        first_block = 2 * n_proj
        first_out = first_block + 2 * n_blocks
        last = first_out + dim // step
        plan = ATT_PLAN
        if DO_COMPUTE:
            for c in att_weight_copies(l)[:-1]:
                pl.when(s == 0)(c.wait)
        if DO_COMM:
            ag5(s, 0)

        def proj(i, carry):
            if DO_COMPUTE:
                pl.when(i % n_proj < n_q)(lambda: project_q(i % n_proj, i // n_proj, s))
                pl.when(i % n_proj == n_q)(lambda: project_kv(i // n_proj, s))
            if DO_COMM:
                pl.when(i == 0)(lambda: ag4(s, 1))

                @pl.when(i == n_proj - 1)
                def _():
                    ag5(s, 1)
                    ag_drain(s, (l == 0) & (s == 0))
            at(i, 0, first_block, plan, todo)
            return carry

        repeat(first_block, proj)
        if DO_COMPUTE:
            for c in fresh_out(s, l):
                c.start()
            for c in cache_copies(kl_hbm, vl_hbm, s):
                c.wait()

        def blk(i, carry):
            if DO_COMPUTE:
                pl.when(i % 2 == 0)(lambda: scores(i // 2, s, l))
                pl.when(i % 2 == 1)(lambda: weigh(i // 2, s))
            at(first_block + i, first_block, first_out, plan, todo)
            return carry

        repeat(2 * n_blocks, blk)
        if DO_COMPUTE:
            for c in fresh_out(s, l):
                c.wait()

            @pl.when((l == 0) & (s == 0))
            def _():
                for c in cache_copies(kl_hbm, vl_hbm, 1):
                    c.start()

            @pl.when(l + s == 1)
            def _():
                for c in cache_copies(kg_hbm, vg_hbm, l):
                    c.start()
            pl.when(s == 0)(att_weight_copies(l)[-1].wait)
        if DO_COMM:
            ag_own(t)

        def out_body(i, carry):
            if DO_COMPUTE:
                out_tile(i, s)
            for j in range(step // swap_step):
                swap_columns(s, None, i * step + j * swap_step, swap_step)
            at(first_out + i, first_out, last, plan, todo)
            return carry

        repeat(dim // step, out_body)
        if DO_COMPUTE:
            @pl.when((s == 1) & (l == 0))
            def _():
                for c in att_weight_copies(1):
                    c.start()
        if DO_COMM:
            leave(s)
        rest(plan, todo, last)
        if DO_COMM:
            pl.when(reduce)(lambda: rs_drain(t))

    def mlp_phase(l, s):
        t = 1 - s
        m0 = (2 * l + s) * per_phase
        gather = (l == 0) | (s == 0)
        todo = events(t, 4 * l + 1 + 2 * s, l >= 0, gather)
        first_down = n_up + 2
        last = first_down + n_pairs
        plan = MLP_PLAN
        if DO_COMM:
            ag5(s, 0)

        def halves(i, carry):
            if DO_COMPUTE:
                m = m0 + 2 * i

                @pl.when(i < 2)
                def _():
                    wait_up_tile(m % SLOTS)
                    wait_up_tile((m + 1) % SLOTS)
                up_half(i % 2, i // 2, s, m0)

                @pl.when(i >= 2)
                def _():
                    next_tile(m - 4)
                    next_tile(m - 3)
            if DO_COMM:
                pl.when(i == 0)(lambda: ag4(s, 1))

                @pl.when(i == 1)
                def _():
                    ag5(s, 1)
                    ag_drain(s, l < 0)
            at(i, 0, 4, plan, todo)
            return carry

        repeat(4, halves)

        def ups(jj, carry):
            if DO_COMPUTE:
                up_tile(jj, s, m0)
            at(2 + jj, 4, first_down, plan, todo)
            return carry

        repeat(n_up, ups, 2)

        swap_step = min(SWAP, dim)
        every = swap_step // (DOWN * TILE)

        @pl.when(gather)
        def _():
            def downs(n, carry):
                if DO_COMPUTE:
                    down_pair(n, s, m0)
                if DO_COMM:
                    pl.when(n == every - 1)(lambda: ag_own(t))
                pl.when(n % every == every - 1)(lambda: swap_columns(s, None, n // every * swap_step, swap_step))
                at(first_down + n, first_down, last, plan, todo)
                return carry

            repeat(n_pairs, downs)
            if DO_COMM:
                leave(s)
            rest(plan, todo, last)

        @pl.when(jnp.logical_not(gather))
        def _():
            rare = n_pairs // 2
            if DO_COMM:
                rest(plan[:4], todo, first_down)
                for dev in partners:
                    pl.semaphore_signal(credit, inc=1, device_id=dev, device_id_type=MESH_ID)
            for u in PAIR:
                def downs(n, carry):
                    if DO_COMPUTE:
                        down_pair(u * n_pairs + n, s, m0, u)
                    if DO_COMM:
                        if u == 0:
                            pl.when(n == rare - 1)(lambda: pl.semaphore_wait(credit, len(partners)))
                        pl.when(n % rare == rare - 1)(lambda: swap_columns(s, u, n // rare * (rare * DOWN * TILE), rare * DOWN * TILE))
                        if u == 1:
                            @pl.when(n == min(1, n_pairs - 1))
                            def _():
                                rs1(s, 0, True)
                                rs2(s, 0, True)
                            pl.when(n == min(LAST_RS3, n_pairs - 1))(lambda: rs3(s, 0))
                    return carry

                repeat(n_pairs, downs)
            if DO_COMM:
                rs1(s, 1, True)
                rs2(s, 1, True)
        if DO_COMM:
            rs_drain(t)

    xcopy = pltpu.make_async_copy(x_hbm, xs, s_x)
    xcopy.start()
    barrier = pltpu.get_barrier_semaphore()
    for dev in partners:
        pl.semaphore_signal(barrier, inc=1, device_id=dev, device_id_type=MESH_ID)

    def first_norm(s, u):
        def body(hh, carry):
            v = xs[s, u, rows(hh)].astype(F32)
            g[s, me, u, rows(hh)] = (v * inv_rms(v) * (1.0 + norm_row(0))).astype(BF16)
            return carry

        repeat(2, body)

    xcopy.wait()
    first_norm(0, 0)
    pl.semaphore_wait(barrier, len(partners))
    for u in PAIR:
        if u == 1:
            first_norm(0, 1)
        if DO_COMM:
            ag_out(0, u, 0)
            ag_d2d(0, u, 0, core).start()
    if DO_COMPUTE:
        for c in att_weight_copies(0) + cache_copies(kl_hbm, vl_hbm, 0):
            c.start()
        for m in range(SLOTS):
            start_tile(jnp.int32(m))
    for u in PAIR:
        first_norm(1, u)
    for s in PAIR:
        shape = cos_ref.shape[1:]
        pos = start_ref[s] + sum(n * lax.broadcasted_iota(jnp.int32, shape, i) for i, n in enumerate((2 * half, half, 1)))
        angle = pos.astype(F32) * freq_ref[...]
        cos_ref[s] = jnp.cos(angle)
        sin = jnp.sin(angle)
        sin_ref[s] = jnp.where(lax.broadcasted_iota(jnp.int32, shape, 3) < hd // 2, -sin, sin)
        bias[s] = jnp.where(lax.broadcasted_iota(jnp.int32, (1, past), 1) < start_ref[s], 0.0, MASKED)
    if DO_COMM:
        for u in PAIR:
            ag_gone(0, u, 0)
            ag_out(0, u, 1)
        for u in PAIR:
            ag2(0, u)
        for u in PAIR:
            ag3(0, u)
        ag4(0, 0)
        ag_own(0)
        for u in PAIR:
            ag1(1, u)

    def layer(l, carry):
        def att(s, carry):
            att_phase(l, s)
            return carry

        def mlp(s, carry):
            mlp_phase(l, s)
            return carry

        repeat(2, att)
        repeat(2, mlp)
        return carry

    repeat(2, layer)

    out = [pltpu.make_async_copy(xs.at[s, u], xo_hbm.at[s, u], s_xo.at[s, u]) for s in PAIR for u in PAIR]
    out[0].start()
    out[1].start()
    if DO_COMM:
        rs3(1, 1)
    for u in PAIR:
        if DO_COMM:
            rs4_wait(1, u, True)
            finish(1, u, 7, False)
        out[2 + u].start()
    if DO_COMM:
        rs_drain(1, PAIR)
    for copy in out:
        copy.wait()


def run_layers(x, start, freq, norms, kl, vl, kg, vg, wq, wk, wv, wo, wg, wu, wd):
    seqs, _, half, dim = x.shape
    past, hd = kl.shape[1], kl.shape[2]
    chunk = kg.shape[1] - past
    n_q = wq.shape[2] // TILE
    devices = chunk // (2 * half)
    ring = pltpu.VMEM((2, 3, half // 2, dim), BF16)
    keys = pltpu.VMEM((past + chunk, hd), BF16)
    whole = pltpu.VMEM((2, devices, 2, half, dim), BF16)
    table = pltpu.VMEM((2, devices, 2, half, hd), F32)

    def dmas(*shape):
        return pltpu.SemaphoreType.DMA(shape)

    scratch = [
        whole, whole,
        pltpu.VMEM((4, 2, half, dim), BF16),
        ring, ring,
        pltpu.VMEM(x.shape, BF16),
        table, table,
        pltpu.VMEM((2, 1, past), F32),
        pltpu.VMEM((n_q + 1, dim, TILE), BF16),
        pltpu.VMEM(wo.shape[1:], BF16),
        pltpu.VMEM((SLOTS, max(dim, DOWN * wd.shape[1]), TILE), BF16),
        pltpu.VMEM((devices, 2, half, wg.shape[2]), BF16),
        pltpu.VMEM((wq.shape[2] // hd, devices, 2, half, hd), BF16),
        pltpu.VMEM((chunk, wq.shape[2]), BF16),
        keys, keys,
        pltpu.VMEM((QROWS, past + chunk), F32),
        pltpu.VMEM((QROWS, hd), F32),
        pltpu.SemaphoreType.DMA, dmas(n_q + 3), dmas(SLOTS, DOWN), dmas(2), dmas(2), dmas(2, 2), pltpu.SemaphoreType.REGULAR,
    ]
    chips = [dmas(2, 2, 3)] * 2
    cores = [dmas(2, 2, 4)] * 2
    sends = [dmas(2, 2, 2, 3)]
    scratch += cores + chips + sends + sends + chips + cores
    return pl.pallas_call(
        layers_kernel,
        out_shape=(jax.ShapeDtypeStruct(x.shape, BF16),) + (jax.ShapeDtypeStruct((2, seqs, chunk, hd), BF16),) * 2,
        in_specs=[ANY, SMEM, VMEM, VMEM] + [ANY] * 11,
        out_specs=(ANY,) * 3,
        scratch_shapes=scratch,
        compiler_params=pltpu.CompilerParams(collective_id=0, has_side_effects=True, vmem_limit_bytes=LAYERS_LIMIT),
        name='layers',
    )(x, start, freq, norms, kl, vl, kg, vg, wq, wk, wv, wo, wg, wu, wd)


def cache_kernel(start_ref, x, k_new, v_new, kl, vl, kg, vg, x_o, kl_o, vl_o, kg_o, vg_o, xbuf, buf, fresh, s_x, s_in, s_fr, s_out):
    chunk = k_new.shape[2]
    window = kl.shape[1]
    lead = fresh.shape[1] - chunk
    n_buf = buf.shape[0]
    jobs = []
    for b in range(kl.shape[0]):
        for l, pairs in enumerate((((kl, k_new, kl_o), (vl, v_new, vl_o)), ((kg, k_new, kg_o), (vg, v_new, vg_o)))):
            jobs += [(src, new, dst, l, b) for src, new, dst in pairs]

    def load(i):
        src, new, _, l, b = jobs[i]
        k = i % n_buf
        return (pltpu.make_async_copy(src.at[b], buf.at[k, pl.ds(0, src.shape[1])], s_in.at[k]),
                pltpu.make_async_copy(new.at[l, b], fresh.at[k, pl.ds(0, chunk)], s_fr.at[k]))

    def store(i):
        src, _, dst, _, b = jobs[i]
        k = i % n_buf
        return pltpu.make_async_copy(buf.at[k, pl.ds(0, src.shape[1])], dst.at[b], s_out.at[k])

    x_in = pltpu.make_async_copy(x, xbuf, s_x)
    x_out = pltpu.make_async_copy(xbuf, x_o, s_x)
    x_in.start()
    for i in range(n_buf):
        for c in load(i):
            c.start()
    x_in.wait()
    x_out.start()
    for i, (_, _, _, l, b) in enumerate(jobs):
        k = i % n_buf
        for c in load(i):
            c.wait()
        start = start_ref[b]
        r = start % lead
        at = pl.multiple_of(start - r, lead)
        rolled = pltpu.roll(fresh[k].astype(F32), r, 0)
        row = lax.broadcasted_iota(jnp.int32, rolled.shape, 0)
        old = buf[k, pl.ds(at, chunk + lead)].astype(F32)
        buf[k, pl.ds(at, chunk + lead)] = jnp.where((row >= r) & (row < r + chunk), rolled, old).astype(BF16)
        if l == 0:
            over = buf[k, pl.ds(window, chunk)].astype(F32)
            row = lax.broadcasted_iota(jnp.int32, over.shape, 0)
            head = buf[k, pl.ds(0, chunk)].astype(F32)
            buf[k, pl.ds(0, chunk)] = jnp.where(row < start + chunk - window, over, head).astype(BF16)
        store(i).start()
        if i >= 1 and i - 1 + n_buf < len(jobs):
            store(i - 1).wait()
            for c in load(i - 1 + n_buf):
                c.start()
    for i in range(max(0, len(jobs) - n_buf), len(jobs)):
        store(i).wait()
    x_out.wait()


def write_caches(start, x, k_new, v_new, kl, vl, kg, vg):
    hd = kl.shape[2]
    chunk = k_new.shape[2]
    lead = 16
    depth = max(kl.shape[1] + chunk, kg.shape[1]) + lead
    n_buf = 8
    dmas = pltpu.SemaphoreType.DMA((n_buf,))
    return pl.pallas_call(
        cache_kernel,
        out_shape=tuple(jax.ShapeDtypeStruct(c.shape, BF16) for c in (x, kl, vl, kg, vg)),
        in_specs=[SMEM] + [ANY] * 7,
        out_specs=(ANY,) * 5,
        scratch_shapes=[pltpu.VMEM(x.shape, BF16), pltpu.VMEM((n_buf, depth, hd), BF16), pltpu.VMEM((n_buf, chunk + lead, hd), BF16),
                        pltpu.SemaphoreType.DMA, dmas, dmas, dmas],
        compiler_params=pltpu.CompilerParams(vmem_limit_bytes=VMEM_LIMIT),
        name='write_caches',
    )(start, x, k_new, v_new, kl, vl, kg, vg)


def solution(mesh):
    act_spec = P('dp', 'tp', None)
    cache_spec = P('dp', None, 'tp', None)
    col_spec = P(None, None, 'tp')
    row_spec = P(None, 'tp', None)
    arg_specs = (act_spec, P('dp'), cache_spec, cache_spec, cache_spec, cache_spec, P(), col_spec, col_spec, col_spec, row_spec, col_spec, col_spec, row_spec)
    result_specs = (act_spec, cache_spec, cache_spec, cache_spec, cache_spec)

    def device_step(x, start, k_local, v_local, k_global, v_global, norms, w_q, w_k, w_v, w_o, w_gate, w_up, w_down):
        hd = k_local.shape[3]
        freq = ROPE_BASE ** (np.arange(hd // 2) * (-2.0 / hd))
        freq = jnp.asarray(np.concatenate([freq, freq])[None], F32)
        flat = [c.reshape(c.shape[0], c.shape[1], hd) for c in (k_local, v_local, k_global, v_global)]
        x4 = x.reshape(x.shape[0], 2, x.shape[1] // 2, x.shape[2])
        x_out, k_new, v_new = run_layers(x4, start, freq, norms, *flat, w_q, w_k, w_v, w_o, w_gate, w_up, w_down)
        x_out = x_out.reshape(x.shape)
        x_out, *caches = write_caches(start, x_out, k_new, v_new, *flat)
        return (x_out,) + tuple(c.reshape(c.shape[0], c.shape[1], 1, hd) for c in caches)

    return jax.shard_map(device_step, mesh=mesh, in_specs=arg_specs, out_specs=result_specs, check_vma=False)
```

time: 328 us -> 312 us (0.951)
  Pallas kernels: 327 us -> 311 us
    pallas_call x1, Pallas kernels: 319 us -> 302 us  [run_layers(): pl.pallas_call(layers_kernel, out_shape=(jax.ShapeDtypeStruct(x.shape, BF...]
where the time goes in v2:
time: 312 us; the launch traced here: 311 us
  Pallas kernels  311 us (100%)
    pallas_call x1, Pallas kernels, run_layers(): pl.pallas_call(layers_kernel, out_shape=(jax.ShapeDtypeStruct(x.shape, BF...  302 us
    pallas_call x1, Pallas kernels, write_caches(): pl.pallas_call(cache_kernel, out_shape=tuple((jax.ShapeDtypeStruct(c.shap...  8.44 us

profile of v2, /device:TPU:81, one launch (start us, length us, event | category | flops | bytes accessed | tf_op | source)
XLA Modules:
  0.0 311.5 jit_solution(4065424514848558969)
XLA Ops:
  0.6 302.2 %layers.1 = (bf16[2,2,32,4096]{3,2,1,0:T(8,128)(2,1)}, bf16[2,2,512,128]{3,2,1,0:T(8,128)(2,1)}, bf16[2,2,512,128]{3,2,1,0:T(8,128)(2,1)}) custom-call(bf16[2,2,32,4096]{3,2,1,0:T(8,128)(2,1)} %bitcast.26, s32[2]{0:T(128)} %start_ref.3, f32[1,128]{1,0:T(1,128)} %constant.2.clone.freq_ref, f32[2,4,4096]{2,1,0:T(4,128)} %norms_ref.1, ...), custom_call_target="tpu_custom_call" | custom-call | tf_op jit(solution)/shard_map/layers/pallas_call | solution.py:765
  302.9 8.4 %write_caches.1 = (bf16[2,64,4096]{2,1,0:T(8,128)(2,1)}, bf16[2,4096,128]{2,1,0:T(8,128)(2,1)}, bf16[2,4096,128]{2,1,0:T(8,128)(2,1)}, bf16[2,4608,128]{2,1,0:T(8,128)(2,1)}, bf16[2,4608,128]{2,1,0:T(8,128)(2,1)}) custom-call(s32[2]{0:T(128)} %start_ref.3, bf16[2,64,4096]{2,1,0:T(8,128)(2,1)} %bitcast.27, bf16[2,2,512,128]{3,2,1,0:T(8,128)(2,1)} %get-tuple-element.14.k_new, ...), custom_call_target="tpu_custom_call" | custom-call | tf_op jit(solution)/shard_map/write_caches/pallas_call | solution.py:838

commit v3 on v2

--- a/solution.py
+++ b/solution.py
@@ -24,27 +24,35 @@
 TILE = 256
 SLOTS = 5
 DOWN = 2
-QROWS = 256
+SCORE_KEYS = 256
 KEYS = 512
 OUT = 2048
 VMEM_LIMIT = 67_000_000
 LAYERS_LIMIT = 67_000_000
 SWAP = 1024
-ATT_PLAN = (4, 10, 12, 16, 19, 21, 22, 23, 24)
-MLP_PLAN = (2, 5, 6, 8, 10, 11, 13, 15, 16)
-LAST_RS3 = 7
+ATT_PLAN = ((2, 4), (10, 11), (7, 9), (14, 17), (14, 19), (18, 21), (19, 23), (21, 24), (24, 26))
+MLP_PLAN = ((1, 2), (6, 6), (4, 5), (8, 8), (9, 10), (11, 11), (13, 13), (15, 15), (16, 16))
+LEAVE = 4
+GROUP = 2
+HOLD_NS = 1000
 SWAP_ORDER = (2, 1, 3, 0)
 DO_COMPUTE = True
 DO_COMM = True
 
 PAIR = range(2)
+LATER = (1, 2)
+
+
+def mirror(table):
+    return tuple(((4 - r) % 4, 1 - hh) for r, hh in table)
+
 
 RS_RIGHT = ((2, 0), (1, 1), (1, 0))
-RS_LEFT = ((2, 1), (3, 0), (3, 1))
+RS_LEFT = mirror(RS_RIGHT)
 AG_RIGHT = ((0, 0), (0, 1), (3, 0))
-AG_LEFT = ((0, 1), (0, 0), (1, 1))
+AG_LEFT = mirror(AG_RIGHT)
 AG_FROM_LEFT = ((3, 0), (3, 1), (2, 0))
-AG_FROM_RIGHT = ((1, 1), (1, 0), (2, 1))
+AG_FROM_RIGHT = mirror(AG_FROM_LEFT)
 
 
 def repeat(n, body, low=0):
@@ -65,11 +73,11 @@
                   g, y, rb, ring_l, ring_r, xs, cos_ref, sin_ref, bias, wqkv, wo, slots, h_sc, q_sc, o_sc, kbuf, vbuf, t_sc, mx_sc,
                   s_x, s_attw, s_slot, s_kv, s_kvo, s_xo, credit,
                   rs_ds, rs_dr, rs_rl, rs_rr, rs_sr, ag_sr, ag_rl, ag_rr, ag_ds, ag_dr):
-    devices, half, dim = g.shape[1], g.shape[3], g.shape[4]
+    _, devices, _, half, dim = g.shape
     chunk = devices * 2 * half
     piece = half // 2
-    hd = kbuf.shape[1]
-    past = kbuf.shape[0] - chunk
+    keys, hd = kbuf.shape
+    past = keys - chunk
     n_q = wq_hbm.shape[2] // TILE
     heads = wq_hbm.shape[2] // hd
     ffn = wg_hbm.shape[2]
@@ -78,9 +86,8 @@
     n_pairs = n_down // DOWN
     per_phase = 2 * n_up + n_pairs
     n_tiles = 4 * per_phase + n_pairs
-    n_blocks = heads * chunk // QROWS
-    per_head = chunk // QROWS
-    owners = devices // per_head
+    out_step = min(OUT, dim)
+    swap_step = min(SWAP, dim)
     c1 = (hd ** -0.5) / SOFT_CAP
     c2 = SOFT_CAP * LOG2E
 
@@ -150,8 +157,7 @@
             pltpu.make_async_copy(wd_hbm.at[0, :, pl.ds(0, TILE)], slots.at[slot, pl.ds(i * ffn, ffn)], s_slot.at[slot, i]).wait()
 
     def swap(s, u, r, cols):
-        which, i = (slice(None), 0) if u is None else (u, u)
-        return push(y.at[s, owner(r, 1 - core), which, :, cols], rb.at[r, which, :, cols], rs_ds.at[s, i, r], rs_dr.at[s, i, r], sibling)
+        return push(y.at[s, owner(r, 1 - core), u, :, cols], rb.at[r, u, :, cols], rs_ds.at[s, u, r], rs_dr.at[s, u, r], sibling)
 
     def swap_columns(s, u, first, size):
         if DO_COMM:
@@ -179,27 +185,19 @@
 
         repeat(dim // step, body)
 
-    def fold(s, u, r, apart):
-        if apart:
-            swapped(s, u, r).wait_recv()
-        elif u == 0:
-            swapped(s, None, r).wait_recv()
+    def fold(s, u, r):
+        swapped(s, u, r).wait_recv()
         add_in(y.at[s, owner(r, core), u], rb.at[r, u])
 
-    def rs1(s, u, apart=False):
-        fold(s, u, 2, apart)
+    def rs1(s, u):
+        fold(s, u, 2)
         rs_right(s, u, 0).start()
         rs_left(s, u, 0).start()
 
-    def rs2(s, u, apart=False):
-        hold = apart and u == 1
-        fold(s, u, 1, apart)
-        if not hold:
-            rs_right(s, u, 1).start()
-        fold(s, u, 3, apart)
-        if hold:
-            rs_gone(s, u, 0)
-            rs_right(s, u, 1).start()
+    def rs2(s, u):
+        fold(s, u, 1)
+        rs_right(s, u, 1).start()
+        fold(s, u, 3)
         rs_left(s, u, 1).start()
 
     def rs3(s, u):
@@ -210,27 +208,19 @@
         add_in(y.at[s, owner(3, core), u, rows(1)], ring_r.at[u, 0])
         rs_left(s, u, 2).start()
 
-    def rs4_wait(s, u, apart=False):
-        if apart:
-            swapped(s, u, 0).wait_recv()
-        elif u == 0:
-            swapped(s, None, 0).wait_recv()
-        for k in (1, 2):
+    def rs4_wait(s, u):
+        swapped(s, u, 0).wait_recv()
+        for k in LATER:
             rs_right(s, u, k).wait_recv()
             rs_left(s, u, k).wait_recv()
 
-    def rs_gone(s, u, k):
-        rs_right(s, u, k).wait_send()
-        rs_left(s, u, k).wait_send()
-
-    def rs_drain(s, halves=(None,)):
-        for u in halves:
+    def rs_drain(s):
+        for u in PAIR:
             for r in range(4):
                 swapped(s, u, r).wait_send()
-        for u in PAIR:
             for k in range(3):
-                if None in halves or u == 0 or k > 0:
-                    rs_gone(s, u, k)
+                rs_right(s, u, k).wait_send()
+                rs_left(s, u, k).wait_send()
 
     def norm_row(i):
         return norms_ref[i // 4, pl.ds(i % 4, 1)]
@@ -314,7 +304,7 @@
     def ag_drain(t, first):
         for u in PAIR:
             pl.when(jnp.logical_not(first))(lambda: ag_gone(t, u, 0))
-            for k in (1, 2):
+            for k in LATER:
                 ag_gone(t, u, k)
             for r in range(4):
                 ag_d2d(t, u, r, core).wait_send()
@@ -344,31 +334,32 @@
         return [pltpu.make_async_copy(buf.at[pl.ds(past, chunk)], out.at[l, s], s_kvo.at[i])
                 for i, (buf, out) in enumerate(((kbuf, kn_hbm), (vbuf, vn_hbm)))]
 
-    def scores(b, s, l):
-        tok = (b % per_head) * QROWS
-        diff = lax.broadcasted_iota(jnp.int32, (QROWS, KEYS), 1) - lax.broadcasted_iota(jnp.int32, (QROWS, KEYS), 0)
-        oldest = jnp.where(l == 0, start_ref[s] - past, -past) + tok
-        q = q_sc[b // per_head, pl.ds(b % per_head * owners, owners)].reshape(QROWS, hd)
+    def scores(head, u, s, l):
+        row = lax.broadcasted_iota(jnp.int32, (chunk // 2, SCORE_KEYS), 0)
+        token = row + jnp.bitwise_and(row, -half) + u * half
+        diff = lax.broadcasted_iota(jnp.int32, (chunk // 2, SCORE_KEYS), 1) - token
+        oldest = jnp.where(l == 0, start_ref[s] - past, -past)
+        q = rows_of(q_sc[head, :, u])
         top = None
-        for kb in range((past + chunk) // KEYS):
-            first = kb * KEYS
-            cols = pl.ds(first, KEYS)
-            t = jnp.tanh(dot_nt(q, kbuf[cols]) * c1)
+        for kb in range((past + chunk) // SCORE_KEYS):
+            first = kb * SCORE_KEYS
+            cols = pl.ds(first, SCORE_KEYS)
+            t = jnp.tanh(dot_nt(q, kbuf[cols]) * c1) * c2
             if past // 2 <= first < past:
                 t = t + bias[s, :, cols]
             if first < chunk:
                 t = jnp.where(diff > oldest - first, t, MASKED)
             if first >= past:
-                t = jnp.where(diff <= tok - (first - past), t, MASKED)
+                t = jnp.where(diff <= past - first, t, MASKED)
             t_sc[:, cols] = t
-            for i in range(KEYS // hd):
+            for i in range(SCORE_KEYS // hd):
                 ti = t[:, i * hd:(i + 1) * hd]
                 top = ti if top is None else jnp.maximum(top, ti)
         mx_sc[...] = top
 
-    def weigh(b, s):
-        mc = jnp.max(mx_sc[...], axis=-1, keepdims=True) * c2
-        mc = jnp.broadcast_to(mc, (QROWS, hd))
+    def weigh(head, u):
+        mc = jnp.max(mx_sc[...], axis=-1, keepdims=True)
+        mc = jnp.broadcast_to(mc, (chunk // 2, hd))
         n_kb = (past + chunk) // KEYS
         total = acc = None
         pvs = []
@@ -378,19 +369,18 @@
                 mc = jnp.maximum(mc, jnp.minimum(pvs[kb - DIST], LOWEST))
             ps = []
             for i in range(KEYS // hd):
-                pi = jnp.exp2(t_sc[:, pl.ds(kb * KEYS + i * hd, hd)] * c2 - mc)
+                pi = jnp.exp2(t_sc[:, pl.ds(kb * KEYS + i * hd, hd)] - mc)
                 total = pi if total is None else total + pi
                 ps.append(pi.astype(BF16))
             pv = dot(jnp.concatenate(ps, axis=1), vbuf[cols])
             pvs.append(pv)
             acc = pv if acc is None else acc + pv
         o = acc / jnp.sum(total, axis=-1, keepdims=True)
-        o_sc[pl.ds(pl.multiple_of((b % per_head) * QROWS, QROWS), QROWS), pl.ds(pl.multiple_of(b // per_head * hd, hd), hd)] = o.astype(BF16)
-
-    def out_tile(i, s):
-        step = min(OUT, dim)
-        cols = columns(i * step, step)
-        y[s, :, :, :, cols] = dot(o_sc[...], wo[:, cols]).astype(BF16).reshape(devices, 2, half, step)
+        o_sc[:, u, :, pl.ds(pl.multiple_of(head * hd, hd), hd)] = o.astype(BF16).reshape(devices, half, hd)
+
+    def out_tile(i, u, s):
+        cols = columns(i * out_step, out_step)
+        y[s, :, u, :, cols] = dot(rows_of(o_sc[:, u]), wo[:, cols]).astype(BF16).reshape(devices, half, out_step)
 
     def gated(x, sa, sb):
         return (jax.nn.gelu(dot(x, slots[sa, pl.ds(0, dim)]), approximate=True) * dot(x, slots[sb, pl.ds(0, dim)])).astype(BF16)
@@ -408,76 +398,68 @@
         next_tile(m)
         next_tile(m + 1)
 
-    def down_pair(n, s, m0, u=None):
+    def down_pairs(n, count, s, m0, u=None):
         m = m0 + 2 * n_up + n
-        slot = m % SLOTS
-        wait_down_pair(slot)
-        for i in range(DOWN):
+        for i in range(count):
+            wait_down_pair((m + i) % SLOTS)
+        for i in range(count * DOWN):
             cols = columns((n % n_pairs * DOWN + i) * TILE, TILE)
-            w = slots[slot, pl.ds(i * ffn, ffn)]
+            w = slots[(m + i // DOWN) % SLOTS, pl.ds(i % DOWN * ffn, ffn)]
             if u is None:
                 y[s, :, :, :, cols] = dot(h_sc[...].reshape(chunk, ffn), w).astype(BF16).reshape(devices, 2, half, TILE)
             else:
                 y[s, :, u, :, cols] = dot(rows_of(h_sc[:, u]), w).astype(BF16).reshape(devices, half, TILE)
-        next_tile(m)
-
-    def events(t, post, reduce, gather):
-        def reduced(u):
-            @pl.when(reduce)
-            def _():
-                rs4_wait(t, u)
-
-                @pl.when(gather)
-                def _():
-                    finish(t, u, post, True)
-                    ag1(t, u)
-
-                @pl.when(jnp.logical_not(gather))
-                def _():
-                    finish(t, u, post, False)
-
-        def if_reduce(*what):
-            def run():
-                @pl.when(reduce)
-                def _():
-                    for f, u in what:
-                        f(t, u)
-            return run
+        for i in range(count):
+            next_tile(m + i)
+
+    def settle(t, u, post, gather):
+        rs4_wait(t, u)
+
+        @pl.when(gather)
+        def _():
+            finish(t, u, post, True)
+            ag1(t, u)
+
+        @pl.when(jnp.logical_not(gather))
+        def _():
+            finish(t, u, post, False)
+
+    def events(t, post, reduce, early, gather):
+        def onward():
+            rs3(t, 0)
+            pl.when(jnp.logical_not(early))(lambda: rs2(t, 1))
+
+        def if_reduce(what):
+            return lambda: pl.when(reduce)(what)
 
         def if_gather(f, u):
             return lambda: pl.when(gather)(lambda: f(t, u))
 
-        return (if_reduce((rs3, 0), (rs2, 1)), if_reduce((rs3, 1)), lambda: reduced(0), lambda: reduced(1),
+        return (if_reduce(onward), if_reduce(lambda: settle(t, 0, post, gather)), if_reduce(lambda: rs3(t, 1)),
+                if_reduce(lambda: settle(t, 1, post, gather)),
                 if_gather(ag2, 0), if_gather(ag3, 0), if_gather(ag2, 1), if_gather(ag3, 1), if_gather(ag4, 0))
 
-    def at(step, low, high, plan, todo):
+    def at(step, low, high, early, plan, todo):
         if DO_COMM:
-            for when, what in zip(plan, todo):
-                if low <= when < high:
-                    pl.when(step == when)(what)
-
-    def leave(s):
-        rs1(s, 0)
-        rs2(s, 0)
-        rs1(s, 1)
-
-    def rest(plan, todo, last):
-        if DO_COMM:
-            for when, what in zip(plan, todo):
-                if when >= last:
-                    what()
+            for (soon, late), what in sorted(zip(plan, todo), key=lambda e: e[0][1]):
+                if low <= soon < high or low <= late < high:
+                    pl.when(step == jnp.where(early, soon, late))(what)
+
+    def rest(early, plan, todo, last):
+        for (soon, late), what in zip(plan, todo):
+            if max(soon, late) >= last:
+                pl.when(jnp.where(early, soon, late) >= last)(what)
 
     def att_phase(l, s):
         t = 1 - s
         reduce = (l > 0) | (s > 0)
-        todo = events(t, 4 * l - 1 + 2 * s, reduce, l >= 0)
-        step = min(OUT, dim)
-        swap_step = min(SWAP, dim)
+        early = l == 0
+        todo = events(t, 4 * l - 1 + 2 * s, reduce, early, l >= 0)
         n_proj = n_q + 1
+        n_out = dim // out_step
         first_block = 2 * n_proj
-        first_out = first_block + 2 * n_blocks
-        last = first_out + dim // step
-        plan = ATT_PLAN
+        per_half = 2 * heads + n_out
+        last = first_block + 2 * per_half
         if DO_COMPUTE:
             for c in att_weight_copies(l)[:-1]:
                 pl.when(s == 0)(c.wait)
@@ -495,7 +477,7 @@
                 def _():
                     ag5(s, 1)
                     ag_drain(s, (l == 0) & (s == 0))
-            at(i, 0, first_block, plan, todo)
+            at(i, 0, first_block, early, ATT_PLAN, todo)
             return carry
 
         repeat(first_block, proj)
@@ -504,60 +486,85 @@
                 c.start()
             for c in cache_copies(kl_hbm, vl_hbm, s):
                 c.wait()
-
-        def blk(i, carry):
-            if DO_COMPUTE:
-                pl.when(i % 2 == 0)(lambda: scores(i // 2, s, l))
-                pl.when(i % 2 == 1)(lambda: weigh(i // 2, s))
-            at(first_block + i, first_block, first_out, plan, todo)
-            return carry
-
-        repeat(2 * n_blocks, blk)
-        if DO_COMPUTE:
-            for c in fresh_out(s, l):
-                c.wait()
-
-            @pl.when((l == 0) & (s == 0))
-            def _():
-                for c in cache_copies(kl_hbm, vl_hbm, 1):
-                    c.start()
-
-            @pl.when(l + s == 1)
-            def _():
-                for c in cache_copies(kg_hbm, vg_hbm, l):
-                    c.start()
-            pl.when(s == 0)(att_weight_copies(l)[-1].wait)
-        if DO_COMM:
-            ag_own(t)
-
-        def out_body(i, carry):
-            if DO_COMPUTE:
-                out_tile(i, s)
-            for j in range(step // swap_step):
-                swap_columns(s, None, i * step + j * swap_step, swap_step)
-            at(first_out + i, first_out, last, plan, todo)
-            return carry
-
-        repeat(dim // step, out_body)
+        for u in PAIR:
+            low = first_block + u * per_half
+
+            def blk(i, carry):
+                if DO_COMPUTE:
+                    pl.when(i % 2 == 0)(lambda: scores(i // 2, u, s, l))
+                    pl.when(i % 2 == 1)(lambda: weigh(i // 2, u))
+                at(low + i, low, low + 2 * heads, early, ATT_PLAN, todo)
+                if DO_COMM and u == 1:
+                    @pl.when(early & (i == 1))
+                    def _():
+                        ag_own(t)
+                        swap_columns(s, 0, 0, dim)
+
+                    @pl.when(early & (i == LEAVE))
+                    def _():
+                        rs1(s, 0)
+                        rs2(s, 0)
+                return carry
+
+            repeat(2 * heads, blk)
+            if DO_COMPUTE and u == 0:
+                pl.when(s == 0)(att_weight_copies(l)[-1].wait)
+            if DO_COMPUTE and u == 1:
+                for c in fresh_out(s, l):
+                    c.wait()
+
+                @pl.when((l == 0) & (s == 0))
+                def _():
+                    for c in cache_copies(kl_hbm, vl_hbm, 1):
+                        c.start()
+
+                @pl.when(l + s == 1)
+                def _():
+                    for c in cache_copies(kg_hbm, vg_hbm, l):
+                        c.start()
+            if DO_COMM:
+                if u == 1:
+                    pl.when(jnp.logical_not(early))(lambda: ag_own(t))
+
+            def out_body(i, carry):
+                if DO_COMPUTE:
+                    out_tile(i, u, s)
+                for j in range(out_step // swap_step):
+                    first = i * out_step + j * swap_step
+                    if u == 1:
+                        pl.when(jnp.logical_not(early))(lambda: swap_columns(s, 0, first, swap_step))
+                        swap_columns(s, 1, first, swap_step)
+                at(low + 2 * heads + i, low + 2 * heads, low + per_half, early, ATT_PLAN, todo)
+                return carry
+
+            repeat(n_out, out_body)
         if DO_COMPUTE:
             @pl.when((s == 1) & (l == 0))
             def _():
                 for c in att_weight_copies(1):
                     c.start()
         if DO_COMM:
-            leave(s)
-        rest(plan, todo, last)
-        if DO_COMM:
+            @pl.when(early)
+            def _():
+                rs1(s, 1)
+                rs2(s, 1)
+
+            @pl.when(jnp.logical_not(early))
+            def _():
+                rs1(s, 0)
+                rs2(s, 0)
+                rs1(s, 1)
+            rest(early, ATT_PLAN, todo, last)
             pl.when(reduce)(lambda: rs_drain(t))
 
     def mlp_phase(l, s):
         t = 1 - s
         m0 = (2 * l + s) * per_phase
         gather = (l == 0) | (s == 0)
-        todo = events(t, 4 * l + 1 + 2 * s, l >= 0, gather)
+        early = l + s == 0
+        todo = events(t, 4 * l + 1 + 2 * s, l >= 0, early, gather)
         first_down = n_up + 2
         last = first_down + n_pairs
-        plan = MLP_PLAN
         if DO_COMM:
             ag5(s, 0)
 
@@ -582,7 +589,7 @@
                 def _():
                     ag5(s, 1)
                     ag_drain(s, l < 0)
-            at(i, 0, 4, plan, todo)
+            at(i, 0, 4, early, MLP_PLAN, todo)
             return carry
 
         repeat(4, halves)
@@ -590,57 +597,68 @@
         def ups(jj, carry):
             if DO_COMPUTE:
                 up_tile(jj, s, m0)
-            at(2 + jj, 4, first_down, plan, todo)
+            at(2 + jj, 4, first_down, early, MLP_PLAN, todo)
             return carry
 
         repeat(n_up, ups, 2)
 
-        swap_step = min(SWAP, dim)
         every = swap_step // (DOWN * TILE)
 
         @pl.when(gather)
         def _():
             def downs(n, carry):
                 if DO_COMPUTE:
-                    down_pair(n, s, m0)
+                    down_pairs(n, 1, s, m0)
                 if DO_COMM:
                     pl.when(n == every - 1)(lambda: ag_own(t))
-                pl.when(n % every == every - 1)(lambda: swap_columns(s, None, n // every * swap_step, swap_step))
-                at(first_down + n, first_down, last, plan, todo)
+
+                @pl.when(n % every == every - 1)
+                def _():
+                    for u in PAIR:
+                        swap_columns(s, u, n // every * swap_step, swap_step)
+                at(first_down + n, first_down, last, early, MLP_PLAN, todo)
                 return carry
 
             repeat(n_pairs, downs)
             if DO_COMM:
-                leave(s)
-            rest(plan, todo, last)
+                rs1(s, 0)
+                rs2(s, 0)
+                rs1(s, 1)
+                rest(early, MLP_PLAN, todo, last)
 
         @pl.when(jnp.logical_not(gather))
         def _():
-            rare = n_pairs // 2
             if DO_COMM:
-                rest(plan[:4], todo, first_down)
+                rest(early, MLP_PLAN[:4], todo, first_down)
                 for dev in partners:
                     pl.semaphore_signal(credit, inc=1, device_id=dev, device_id_type=MESH_ID)
+            n_steps = n_pairs // GROUP
+            rare = max(n_steps // 2, 1)
+            width = rare * GROUP * DOWN * TILE
             for u in PAIR:
                 def downs(n, carry):
                     if DO_COMPUTE:
-                        down_pair(u * n_pairs + n, s, m0, u)
+                        down_pairs(u * n_pairs + n * GROUP, GROUP, s, m0, u)
                     if DO_COMM:
                         if u == 0:
                             pl.when(n == rare - 1)(lambda: pl.semaphore_wait(credit, len(partners)))
-                        pl.when(n % rare == rare - 1)(lambda: swap_columns(s, u, n // rare * (rare * DOWN * TILE), rare * DOWN * TILE))
+                        pl.when(n % rare == rare - 1)(lambda: swap_columns(s, u, n // rare * width, width))
                         if u == 1:
-                            @pl.when(n == min(1, n_pairs - 1))
+                            @pl.when(n == 0)
                             def _():
-                                rs1(s, 0, True)
-                                rs2(s, 0, True)
-                            pl.when(n == min(LAST_RS3, n_pairs - 1))(lambda: rs3(s, 0))
+                                rs1(s, 0)
+                                rs2(s, 0)
                     return carry
 
-                repeat(n_pairs, downs)
+                repeat(n_steps, downs)
             if DO_COMM:
-                rs1(s, 1, True)
-                rs2(s, 1, True)
+                rs1(s, 1)
+                rs3(s, 0)
+                fold(s, 1, 1)
+                fold(s, 1, 3)
+                pl.delay(HOLD_NS)
+                rs_right(s, 1, 1).start()
+                rs_left(s, 1, 1).start()
         if DO_COMM:
             rs_drain(t)
 
@@ -713,22 +731,22 @@
     out = [pltpu.make_async_copy(xs.at[s, u], xo_hbm.at[s, u], s_xo.at[s, u]) for s in PAIR for u in PAIR]
     out[0].start()
     out[1].start()
-    if DO_COMM:
-        rs3(1, 1)
     for u in PAIR:
         if DO_COMM:
-            rs4_wait(1, u, True)
+            if u == 1:
+                rs3(1, 1)
+            rs4_wait(1, u)
             finish(1, u, 7, False)
         out[2 + u].start()
     if DO_COMM:
-        rs_drain(1, PAIR)
+        rs_drain(1)
     for copy in out:
         copy.wait()
 
 
 def run_layers(x, start, freq, norms, kl, vl, kg, vg, wq, wk, wv, wo, wg, wu, wd):
     seqs, _, half, dim = x.shape
-    past, hd = kl.shape[1], kl.shape[2]
+    _, past, hd = kl.shape
     chunk = kg.shape[1] - past
     n_q = wq.shape[2] // TILE
     devices = chunk // (2 * half)
@@ -752,10 +770,10 @@
         pltpu.VMEM((SLOTS, max(dim, DOWN * wd.shape[1]), TILE), BF16),
         pltpu.VMEM((devices, 2, half, wg.shape[2]), BF16),
         pltpu.VMEM((wq.shape[2] // hd, devices, 2, half, hd), BF16),
-        pltpu.VMEM((chunk, wq.shape[2]), BF16),
+        pltpu.VMEM((devices, 2, half, wq.shape[2]), BF16),
         keys, keys,
-        pltpu.VMEM((QROWS, past + chunk), F32),
-        pltpu.VMEM((QROWS, hd), F32),
+        pltpu.VMEM((chunk // 2, past + chunk), F32),
+        pltpu.VMEM((chunk // 2, hd), F32),
         pltpu.SemaphoreType.DMA, dmas(n_q + 3), dmas(SLOTS, DOWN), dmas(2), dmas(2), dmas(2, 2), pltpu.SemaphoreType.REGULAR,
     ]
     chips = [dmas(2, 2, 3)] * 2
@@ -774,8 +792,8 @@
 
 
 def cache_kernel(start_ref, x, k_new, v_new, kl, vl, kg, vg, x_o, kl_o, vl_o, kg_o, vg_o, xbuf, buf, fresh, s_x, s_in, s_fr, s_out):
-    chunk = k_new.shape[2]
-    window = kl.shape[1]
+    _, _, chunk, _ = k_new.shape
+    _, window, _ = kl.shape
     lead = fresh.shape[1] - chunk
     n_buf = buf.shape[0]
     jobs = []
@@ -829,8 +847,8 @@
 
 
 def write_caches(start, x, k_new, v_new, kl, vl, kg, vg):
-    hd = kl.shape[2]
-    chunk = k_new.shape[2]
+    _, _, hd = kl.shape
+    _, _, chunk, _ = k_new.shape
     lead = 16
     depth = max(kl.shape[1] + chunk, kg.shape[1]) + lead
     n_buf = 8

time: 312 us -> 309 us (level)
  no operation moved by 1% of the time
where the time goes in v3:
time: 309 us; the launch traced here: 308 us
  Pallas kernels  308 us (100%)
    pallas_call x1, Pallas kernels, run_layers(): pl.pallas_call(layers_kernel, out_shape=(jax.ShapeDtypeStruct(x.shape, BF...  299 us
    pallas_call x1, Pallas kernels, write_caches(): pl.pallas_call(cache_kernel, out_shape=tuple((jax.ShapeDtypeStruct(c.shap...  8.44 us

profile of v3, /device:TPU:81, one launch (start us, length us, event | category | flops | bytes accessed | tf_op | source)
XLA Modules:
  0.0 308.5 jit_solution(6155883481806411801)
XLA Ops:
  0.6 299.2 %layers.1 = (bf16[2,2,32,4096]{3,2,1,0:T(8,128)(2,1)}, bf16[2,2,512,128]{3,2,1,0:T(8,128)(2,1)}, bf16[2,2,512,128]{3,2,1,0:T(8,128)(2,1)}) custom-call(bf16[2,2,32,4096]{3,2,1,0:T(8,128)(2,1)} %bitcast.26, s32[2]{0:T(128)} %start_ref.3, f32[1,128]{1,0:T(1,128)} %constant.2.clone.freq_ref, f32[2,4,4096]{2,1,0:T(4,128)} %norms_ref.1, ...), custom_call_target="tpu_custom_call" | custom-call | tf_op jit(solution)/shard_map/layers/pallas_call | solution.py:783
  299.8 8.4 %write_caches.1 = (bf16[2,64,4096]{2,1,0:T(8,128)(2,1)}, bf16[2,4096,128]{2,1,0:T(8,128)(2,1)}, bf16[2,4096,128]{2,1,0:T(8,128)(2,1)}, bf16[2,4608,128]{2,1,0:T(8,128)(2,1)}, bf16[2,4608,128]{2,1,0:T(8,128)(2,1)}) custom-call(s32[2]{0:T(128)} %start_ref.3, bf16[2,64,4096]{2,1,0:T(8,128)(2,1)} %bitcast.27, bf16[2,2,512,128]{3,2,1,0:T(8,128)(2,1)} %get-tuple-element.14.k_new, ...), custom_call_target="tpu_custom_call" | custom-call | tf_op jit(solution)/shard_map/write_caches/pallas_call | solution.py:856

commit v4 on v3

--- a/solution.py
+++ b/solution.py
@@ -67,10 +67,10 @@
     return lax.dot_general(a, b, (((1,), (1,)), ((), ())), preferred_element_type=F32)
 
 
-def layers_kernel(x_hbm, start_ref, freq_ref, norms_ref, kl_hbm, vl_hbm, kg_hbm, vg_hbm,
+def layers_kernel(x_hbm, start_ref, freq_hbm, norms_hbm, kl_hbm, vl_hbm, kg_hbm, vg_hbm,
                   wq_hbm, wk_hbm, wv_hbm, wo_hbm, wg_hbm, wu_hbm, wd_hbm,
                   xo_hbm, kn_hbm, vn_hbm,
-                  g, y, rb, ring_l, ring_r, xs, cos_ref, sin_ref, bias, wqkv, wo, slots, h_sc, q_sc, o_sc, kbuf, vbuf, t_sc, mx_sc,
+                  g, y, rb, ring_l, ring_r, xs, norms_ref, freq_ref, cos_ref, sin_ref, bias, wqkv, wo, slots, h_sc, q_sc, o_sc, kbuf, vbuf, t_sc, mx_sc,
                   s_x, s_attw, s_slot, s_kv, s_kvo, s_xo, credit,
                   rs_ds, rs_dr, rs_rl, rs_rr, rs_sr, ag_sr, ag_rl, ag_rr, ag_ds, ag_dr):
     _, devices, _, half, dim = g.shape
@@ -358,7 +358,7 @@
         mx_sc[...] = top
 
     def weigh(head, u):
-        mc = jnp.max(mx_sc[...], axis=-1, keepdims=True)
+        mc = jnp.max(mx_sc[...], axis=-1, keepdims=True) + float((past + chunk).bit_length())
         mc = jnp.broadcast_to(mc, (chunk // 2, hd))
         n_kb = (past + chunk) // KEYS
         total = acc = None
@@ -662,8 +662,9 @@
         if DO_COMM:
             rs_drain(t)
 
-    xcopy = pltpu.make_async_copy(x_hbm, xs, s_x)
-    xcopy.start()
+    first = [pltpu.make_async_copy(src, dst, s_x.at[i]) for i, (src, dst) in enumerate(((x_hbm, xs), (norms_hbm, norms_ref), (freq_hbm, freq_ref)))]
+    for copy in first:
+        copy.start()
     barrier = pltpu.get_barrier_semaphore()
     for dev in partners:
         pl.semaphore_signal(barrier, inc=1, device_id=dev, device_id_type=MESH_ID)
@@ -676,7 +677,8 @@
 
         repeat(2, body)
 
-    xcopy.wait()
+    for copy in first:
+        copy.wait()
     first_norm(0, 0)
     pl.semaphore_wait(barrier, len(partners))
     for u in PAIR:
@@ -763,6 +765,7 @@
         pltpu.VMEM((4, 2, half, dim), BF16),
         ring, ring,
         pltpu.VMEM(x.shape, BF16),
+        pltpu.VMEM(norms.shape, F32), pltpu.VMEM(freq.shape, F32),
         table, table,
         pltpu.VMEM((2, 1, past), F32),
         pltpu.VMEM((n_q + 1, dim, TILE), BF16),
@@ -774,7 +777,7 @@
         keys, keys,
         pltpu.VMEM((chunk // 2, past + chunk), F32),
         pltpu.VMEM((chunk // 2, hd), F32),
-        pltpu.SemaphoreType.DMA, dmas(n_q + 3), dmas(SLOTS, DOWN), dmas(2), dmas(2), dmas(2, 2), pltpu.SemaphoreType.REGULAR,
+        dmas(3), dmas(n_q + 3), dmas(SLOTS, DOWN), dmas(2), dmas(2), dmas(2, 2), pltpu.SemaphoreType.REGULAR,
     ]
     chips = [dmas(2, 2, 3)] * 2
     cores = [dmas(2, 2, 4)] * 2
@@ -783,7 +786,7 @@
     return pl.pallas_call(
         layers_kernel,
         out_shape=(jax.ShapeDtypeStruct(x.shape, BF16),) + (jax.ShapeDtypeStruct((2, seqs, chunk, hd), BF16),) * 2,
-        in_specs=[ANY, SMEM, VMEM, VMEM] + [ANY] * 11,
+        in_specs=[ANY, SMEM] + [ANY] * 13,
         out_specs=(ANY,) * 3,
         scratch_shapes=scratch,
         compiler_params=pltpu.CompilerParams(collective_id=0, has_side_effects=True, vmem_limit_bytes=LAYERS_LIMIT),
@@ -791,59 +794,47 @@
     )(x, start, freq, norms, kl, vl, kg, vg, wq, wk, wv, wo, wg, wu, wd)
 
 
-def cache_kernel(start_ref, x, k_new, v_new, kl, vl, kg, vg, x_o, kl_o, vl_o, kg_o, vg_o, xbuf, buf, fresh, s_x, s_in, s_fr, s_out):
+def cache_kernel(start_ref, x, k_new, v_new, kl, vl, kg, vg, x_o, kl_o, vl_o, kg_o, vg_o, xbuf, buf, fresh, turned, s_x, s_in, s_fr, s_out):
     _, _, chunk, _ = k_new.shape
     _, window, _ = kl.shape
-    lead = fresh.shape[1] - chunk
-    n_buf = buf.shape[0]
+    _, size, hd = fresh.shape
+    lead = size - chunk
     jobs = []
-    for b in range(kl.shape[0]):
-        for l, pairs in enumerate((((kl, k_new, kl_o), (vl, v_new, vl_o)), ((kg, k_new, kg_o), (vg, v_new, vg_o)))):
-            jobs += [(src, new, dst, l, b) for src, new, dst in pairs]
-
-    def load(i):
-        src, new, _, l, b = jobs[i]
-        k = i % n_buf
-        return (pltpu.make_async_copy(src.at[b], buf.at[k, pl.ds(0, src.shape[1])], s_in.at[k]),
-                pltpu.make_async_copy(new.at[l, b], fresh.at[k, pl.ds(0, chunk)], s_fr.at[k]))
-
-    def store(i):
-        src, _, dst, _, b = jobs[i]
-        k = i % n_buf
-        return pltpu.make_async_copy(buf.at[k, pl.ds(0, src.shape[1])], dst.at[b], s_out.at[k])
-
+    for b in PAIR:
+        for l, group in enumerate((((kl, k_new, kl_o), (vl, v_new, vl_o)), ((kg, k_new, kg_o), (vg, v_new, vg_o)))):
+            jobs += [(c, new, out, l, b) for c, new, out in group]
+    rows_in = [pltpu.make_async_copy(new.at[l, b], fresh.at[i, pl.ds(0, chunk)], s_fr.at[i]) for i, (_, new, _, l, b) in enumerate(jobs)]
+    loads = [pltpu.make_async_copy(c.at[b], buf.at[i, pl.ds(0, c.shape[1])], s_in.at[i]) for i, (c, _, _, _, b) in enumerate(jobs)]
+    stores = [pltpu.make_async_copy(buf.at[i, pl.ds(0, c.shape[1])], out.at[b], s_out.at[i]) for i, (c, _, out, _, b) in enumerate(jobs)]
     x_in = pltpu.make_async_copy(x, xbuf, s_x)
     x_out = pltpu.make_async_copy(xbuf, x_o, s_x)
-    x_in.start()
-    for i in range(n_buf):
-        for c in load(i):
-            c.start()
-    x_in.wait()
-    x_out.start()
+    for copy in rows_in + loads + [x_in]:
+        copy.start()
     for i, (_, _, _, l, b) in enumerate(jobs):
-        k = i % n_buf
-        for c in load(i):
-            c.wait()
+        rows_in[i].wait()
+        turned[i] = pltpu.roll(fresh[i].astype(F32), start_ref[b] % lead, 0).astype(BF16)
+    row = lax.broadcasted_iota(jnp.int32, (lead, hd), 0)
+    for i, (_, _, _, l, b) in enumerate(jobs):
+        loads[i].wait()
         start = start_ref[b]
         r = start % lead
         at = pl.multiple_of(start - r, lead)
-        rolled = pltpu.roll(fresh[k].astype(F32), r, 0)
-        row = lax.broadcasted_iota(jnp.int32, rolled.shape, 0)
-        old = buf[k, pl.ds(at, chunk + lead)].astype(F32)
-        buf[k, pl.ds(at, chunk + lead)] = jnp.where((row >= r) & (row < r + chunk), rolled, old).astype(BF16)
+        end = pl.ds(pl.multiple_of(at + chunk, lead), lead)
+        first = buf[i, pl.ds(at, lead)].astype(F32)
+        after = buf[i, end].astype(F32)
+        buf[i, pl.ds(at, lead)] = jnp.where(row >= r, turned[i, pl.ds(0, lead)].astype(F32), first).astype(BF16)
+        buf[i, pl.ds(pl.multiple_of(at + lead, lead), chunk - lead)] = turned[i, pl.ds(lead, chunk - lead)]
+        buf[i, end] = jnp.where(row < r, turned[i, pl.ds(chunk, lead)].astype(F32), after).astype(BF16)
         if l == 0:
-            over = buf[k, pl.ds(window, chunk)].astype(F32)
-            row = lax.broadcasted_iota(jnp.int32, over.shape, 0)
-            head = buf[k, pl.ds(0, chunk)].astype(F32)
-            buf[k, pl.ds(0, chunk)] = jnp.where(row < start + chunk - window, over, head).astype(BF16)
-        store(i).start()
-        if i >= 1 and i - 1 + n_buf < len(jobs):
-            store(i - 1).wait()
-            for c in load(i - 1 + n_buf):
-                c.start()
-    for i in range(max(0, len(jobs) - n_buf), len(jobs)):
-        store(i).wait()
-    x_out.wait()
+            over = buf[i, pl.ds(window, chunk)].astype(F32)
+            head = buf[i, pl.ds(0, chunk)].astype(F32)
+            landed = lax.broadcasted_iota(jnp.int32, over.shape, 0) < start + chunk - window
+            buf[i, pl.ds(0, chunk)] = jnp.where(landed, over, head).astype(BF16)
+        stores[i].start()
+    x_in.wait()
+    x_out.start()
+    for copy in stores + [x_out]:
+        copy.wait()
 
 
 def write_caches(start, x, k_new, v_new, kl, vl, kg, vg):
@@ -851,14 +842,15 @@
     _, _, chunk, _ = k_new.shape
     lead = 16
     depth = max(kl.shape[1] + chunk, kg.shape[1]) + lead
-    n_buf = 8
-    dmas = pltpu.SemaphoreType.DMA((n_buf,))
+    jobs = 4 * len(PAIR)
+    dmas = pltpu.SemaphoreType.DMA((jobs,))
+    chunks = pltpu.VMEM((jobs, chunk + lead, hd), BF16)
     return pl.pallas_call(
         cache_kernel,
         out_shape=tuple(jax.ShapeDtypeStruct(c.shape, BF16) for c in (x, kl, vl, kg, vg)),
         in_specs=[SMEM] + [ANY] * 7,
         out_specs=(ANY,) * 5,
-        scratch_shapes=[pltpu.VMEM(x.shape, BF16), pltpu.VMEM((n_buf, depth, hd), BF16), pltpu.VMEM((n_buf, chunk + lead, hd), BF16),
+        scratch_shapes=[pltpu.VMEM(x.shape, BF16), pltpu.VMEM((jobs, depth, hd), BF16), chunks, chunks,
                         pltpu.SemaphoreType.DMA, dmas, dmas, dmas],
         compiler_params=pltpu.CompilerParams(vmem_limit_bytes=VMEM_LIMIT),
         name='write_caches',

time: 309 us -> 309 us (level)
  no operation moved by 1% of the time
where the time goes in v4:
time: 309 us; the launch traced here: 308 us
  Pallas kernels  308 us (100%)
    pallas_call x1, Pallas kernels, run_layers(): pl.pallas_call(layers_kernel, out_shape=(jax.ShapeDtypeStruct(x.shape, BF...  299 us
    pallas_call x1, Pallas kernels, write_caches(): pl.pallas_call(cache_kernel, out_shape=tuple((jax.ShapeDtypeStruct(c.shap...  8.37 us

profile of v4, /device:TPU:81, one launch (start us, length us, event | category | flops | bytes accessed | tf_op | source)
XLA Modules:
  0.0 308.4 jit_solution(17735705199929650780)
XLA Ops:
  0.6 299.3 %layers.1 = (bf16[2,2,32,4096]{3,2,1,0:T(8,128)(2,1)}, bf16[2,2,512,128]{3,2,1,0:T(8,128)(2,1)}, bf16[2,2,512,128]{3,2,1,0:T(8,128)(2,1)}) custom-call(bf16[2,2,32,4096]{3,2,1,0:T(8,128)(2,1)} %bitcast.26, s32[2]{0:T(128)} %start_ref.3, f32[1,128]{1,0:T(1,128)} %constant.2.clone.freq_hbm, f32[2,4,4096]{2,1,0:T(4,128)} %norms_hbm.1, ...), custom_call_target="tpu_custom_call" | custom-call | tf_op jit(solution)/shard_map/layers/pallas_call | solution.py:786
  299.9 8.4 %write_caches.1 = (bf16[2,64,4096]{2,1,0:T(8,128)(2,1)}, bf16[2,4096,128]{2,1,0:T(8,128)(2,1)}, bf16[2,4096,128]{2,1,0:T(8,128)(2,1)}, bf16[2,4608,128]{2,1,0:T(8,128)(2,1)}, bf16[2,4608,128]{2,1,0:T(8,128)(2,1)}) custom-call(s32[2]{0:T(128)} %start_ref.3, bf16[2,64,4096]{2,1,0:T(8,128)(2,1)} %bitcast.27, bf16[2,2,512,128]{3,2,1,0:T(8,128)(2,1)} %get-tuple-element.14.k_new, ...), custom_call_target="tpu_custom_call" | custom-call | tf_op jit(solution)/shard_map/write_caches/pallas_call | solution.py:848

commit v5 on v4

--- a/solution.py
+++ b/solution.py
@@ -22,7 +22,7 @@
 SMEM = pl.BlockSpec(memory_space=pltpu.SMEM)
 
 TILE = 256
-SLOTS = 5
+SLOTS = 6
 DOWN = 2
 SCORE_KEYS = 256
 KEYS = 512
@@ -633,7 +633,7 @@
                 for dev in partners:
                     pl.semaphore_signal(credit, inc=1, device_id=dev, device_id_type=MESH_ID)
             n_steps = n_pairs // GROUP
-            rare = max(n_steps // 2, 1)
+            rare = 1
             width = rare * GROUP * DOWN * TILE
             for u in PAIR:
                 def downs(n, carry):

time: 309 us -> 309 us (level)
  no operation moved by 1% of the time
where the time goes in v5:
time: 309 us
  Pallas kernels  308 us (100%)
    pallas_call x1, Pallas kernels, run_layers(): pl.pallas_call(layers_kernel, out_shape=(jax.ShapeDtypeStruct(x.shape, BF...  300 us
    pallas_call x1, Pallas kernels, write_caches(): pl.pallas_call(cache_kernel, out_shape=tuple((jax.ShapeDtypeStruct(c.shap...  8.37 us

profile of v5, /device:TPU:81, one launch (start us, length us, event | category | flops | bytes accessed | tf_op | source)
XLA Modules:
  0.0 308.8 jit_solution(2026135446279164534)
XLA Ops:
  0.6 299.6 %layers.1 = (bf16[2,2,32,4096]{3,2,1,0:T(8,128)(2,1)}, bf16[2,2,512,128]{3,2,1,0:T(8,128)(2,1)}, bf16[2,2,512,128]{3,2,1,0:T(8,128)(2,1)}) custom-call(bf16[2,2,32,4096]{3,2,1,0:T(8,128)(2,1)} %bitcast.26, s32[2]{0:T(128)} %start_ref.3, f32[1,128]{1,0:T(1,128)} %constant.2.clone.freq_hbm, f32[2,4,4096]{2,1,0:T(4,128)} %norms_hbm.1, ...), custom_call_target="tpu_custom_call" | custom-call | tf_op jit(solution)/shard_map/layers/pallas_call | solution.py:786
  300.3 8.4 %write_caches.1 = (bf16[2,64,4096]{2,1,0:T(8,128)(2,1)}, bf16[2,4096,128]{2,1,0:T(8,128)(2,1)}, bf16[2,4096,128]{2,1,0:T(8,128)(2,1)}, bf16[2,4608,128]{2,1,0:T(8,128)(2,1)}, bf16[2,4608,128]{2,1,0:T(8,128)(2,1)}) custom-call(s32[2]{0:T(128)} %start_ref.3, bf16[2,64,4096]{2,1,0:T(8,128)(2,1)} %bitcast.27, bf16[2,2,512,128]{3,2,1,0:T(8,128)(2,1)} %get-tuple-element.14.k_new, ...), custom_call_target="tpu_custom_call" | custom-call | tf_op jit(solution)/shard_map/write_caches/pallas_call | solution.py:848
